TPU v7x, 32 devices: a whole 2x2x4 slice. The times are simulated.
32 devices in a mesh: row: 8 (over z, core), col: 4 (over y, x).
Axes of the slice: x: 2, y: 2, z: 4, core: 2. Of those that a mesh axis runs over, the one named last changes fastest.
Arguments:
- right_side: float32 [1, 8, 4, 1024], P(None, 'row'), may hold values from -6 to 6
- inverse_t: bfloat16 [1, 8, 1024, 1024], P(None, 'row', 'col'), as said below
- u_factor: bfloat16 [1, 8, 2, 4, 128, 1024], P(None, 'row', None, 'col'), may hold values from -0.25 to 0.25
- v_factor: bfloat16 [1, 8, 2, 4, 128, 1024], P(None, 'row', None, 'col'), may hold values from -0.1875 to 0.1875
- ranks: int32 [1, 8, 2, 4], P(None, 'row', None, 'col'), may hold values from 4 to 128, as said below
Outputs:
- whitened: float32 [1, 8, 4, 1024], P(None, 'row')
- loglik: float32 [1, 8, 4], P(None, 'row')
Inputs may be any that keep to these rules, and one draw needn't show every extreme that they name: Tile (i, j) with j < i uses the first ranks of its factor rows. `inverse_t`: upper triangular with a positive diagonal.
All inputs are finite; a program needn't handle non-finite values.
Results may differ from a plain program's by a relative error of at most 0.0085.
Values sent between devices are 32-bit elements; how exact they have to be, the bound alone decides.
A program may use at most 64 MiB of HBM per device.

v0:
```python
import functools
import math

import jax
import jax.numpy as jnp
from jax import lax
from jax.experimental import pallas as pl
from jax.experimental.pallas import tpu as pltpu
from jax.sharding import PartitionSpec as P

MESH = pl.DeviceIdType.MESH
NT = (((1,), (1,)), ((), ()))
FIRST_SHORT = 4
NEAR = 2


def remote(src, dst, send_sem, recv_sem, device):
    return pltpu.make_async_remote_copy(
        src_ref=src,
        dst_ref=dst,
        send_sem=send_sem,
        recv_sem=recv_sem,
        device_id=device,
        device_id_type=MESH,
    )


def kernel(
    n_row, n_col,
    rhs_hbm, inv_hbm, u_hbm, v_hbm, rank_ref,
    white_ref, lik_ref,
    rhs_ref, inv_ref, u_ref, v_ref,
    y_in, p_out, p_in, y_row, logs, base,
    v_out, v_in, u_out, u_in, fold, w_out, w_in, y_full, y_all,
    in_sem, y_send, y_recv, p_send, p_recv, o_send, o_recv, l_send, l_recv,
    v_send, v_recv, u_send, u_recv, w_send, w_recv, m_send, m_recv, f_send,
):
    row = lax.axis_index("row")
    col = lax.axis_index("col")
    per_col, rank_max, width = u_ref.shape
    nrhs = rhs_ref.shape[0]
    piece = width // n_col
    peers = [lax.rem(col + k, n_col) for k in range(1, n_col)]
    own_slot = row // n_col
    own_home = lax.rem(row, n_col)
    last = n_row - 1

    copies = [
        pltpu.make_async_copy(v_hbm.at[0, 0, :, 0], v_ref, in_sem.at[0]),
        pltpu.make_async_copy(u_hbm.at[0, 0, :, 0], u_ref, in_sem.at[1]),
        pltpu.make_async_copy(inv_hbm.at[0, 0], inv_ref, in_sem.at[2]),
        pltpu.make_async_copy(rhs_hbm.at[0, 0], rhs_ref, in_sem.at[3]),
    ]
    for copy in copies:
        copy.start()

    short = row >= FIRST_SHORT
    feeds = (row + 1 >= FIRST_SHORT) & (row < last)
    long_count = jnp.where(short, row - 1, row)
    long_first = jnp.where(feeds, row + 2, row + 1)
    near_end = jnp.minimum(row + NEAR + 1, n_row)
    relays = col == own_home

    barrier = pltpu.get_barrier_semaphore()

    def greet(i, s):
        pl.semaphore_signal(barrier, inc=1, device_id=(i, s), device_id_type=MESH)

    for peer in peers:
        greet(row, peer)
    greeted = jnp.int32(n_col - 1)

    @pl.when(row < last)
    def _():
        for s in range(n_col):
            greet(row + 1, s)

    greeted = greeted + jnp.where(row < last, n_col, 0)

    @pl.when(row > 0)
    def _():
        for s in range(n_col):
            greet(row - 1, s)

    greeted = greeted + jnp.where(row > 0, n_col, 0)

    for d in range(2, NEAR + 1):

        @pl.when(row + d < n_row)
        def _():
            greet(row + d, own_home)

        greeted = greeted + jnp.where(row + d < n_row, 1, 0)
        fed = (row >= d) & (lax.rem(jnp.maximum(row - d, 0), n_col) == col)

        @pl.when(fed)
        def _():
            for s in range(n_col):
                greet(row - d, s)

        greeted = greeted + jnp.where(fed, n_col, 0)

    def greet_far(i, count):
        greet(i, col)
        return count + 1

    greeted = lax.fori_loop(jnp.where(relays, near_end, n_row), n_row, greet_far, greeted)
    for q in range(per_col):
        j = q * n_col + col

        @pl.when(j < row - NEAR)
        def _():
            greet(j, col)

        greeted = greeted + jnp.where(j < row - NEAR, 1, 0)

    prev_slot = jnp.maximum(row - 1, 0) // n_col
    prev_home = lax.rem(jnp.maximum(row - 1, 0), n_col)
    gives = short & (col == prev_home)
    copies[0].wait()
    copies[1].wait()

    @pl.when(gives)
    def _():
        v_tile = v_ref[prev_slot].astype(jnp.float32)
        keep = lax.broadcasted_iota(jnp.int32, (rank_max, width), 0) < rank_ref[prev_slot]
        u_tile = jnp.where(keep, u_ref[prev_slot].astype(jnp.float32), 0.0)
        for s in range(n_col):
            v_out[s] = v_tile[:, s * piece:(s + 1) * piece]
            u_out[s] = u_tile[:, s * piece:(s + 1) * piece]

    pl.semaphore_wait(barrier, greeted)

    def v_copy(s, i):
        part = pl.ds(s, n_col - s)
        return remote(v_out.at[part], v_in.at[part], v_send.at[s], v_recv, (i, s))

    def u_copy(k, peer):
        return remote(u_out.at[peer], u_in, u_send.at[k], u_recv, (row, peer))

    crosses = short & (lax.rem(row, 2) == 0)

    def by_way(s):
        return crosses & (prev_home != s) & (prev_home + s != n_col - 1)

    def way_copy(cc, s):
        return remote(v_out.at[cc], v_out.at[cc], m_send.at[s], m_recv.at[cc], (row, s))

    @pl.when(gives)
    def _():
        for s in range(n_col):

            @pl.when(by_way(s))
            def _():
                for cc in range(s, n_col):
                    way_copy(cc, s).start()

            @pl.when(jnp.logical_not(by_way(s)))
            def _():
                v_copy(s, row - 1).start()

        for k, peer in enumerate(peers):
            u_copy(k, peer).start()
        u_in[...] = u_out[col]

    @pl.when(by_way(col))
    def _():
        def forward(cc, carry):
            remote(v_out.at[cc], v_out.at[cc], m_send.at[0], m_recv.at[cc], (row, prev_home)).wait_recv()
            remote(v_out.at[cc], v_in.at[cc], f_send, v_recv, (row - 1, col)).start()
            return carry

        lax.fori_loop(col, n_col, forward, 0)

    copies[2].wait()
    copies[3].wait()

    for cc in range(n_col):

        @pl.when(col == cc)
        def _():
            base[...] = rhs_ref[:, cc * piece:(cc + 1) * piece]

    def log_part():
        for cc in range(n_col):

            @pl.when(col == cc)
            def _():
                block = inv_ref[:, cc * piece:(cc + 1) * piece].astype(jnp.float32)
                r_id = lax.broadcasted_iota(jnp.int32, (piece, piece), 0)
                c_id = lax.broadcasted_iota(jnp.int32, (piece, piece), 1)
                diagonal = jnp.sum(jnp.where(r_id == c_id, block, 0.0), axis=0, keepdims=True)
                total = jnp.sum(jnp.log(diagonal), axis=1, keepdims=True)
                logs[cc] = jnp.broadcast_to(total, (1, 128))

        for k, peer in enumerate(peers):
            remote(logs.at[col], logs.at[col], l_send.at[k], l_recv.at[col], (row, peer)).start()

    pl.when(row > 0)(log_part)

    for q in range(per_col):
        j = q * n_col + col

        @pl.when(j < long_count)
        def _():
            near = row - j <= NEAR
            remote(y_in.at[q, 0], y_in.at[q, 0], y_send.at[0], y_recv.at[q, 0], (j, col)).wait_recv()

            @pl.when(near)
            def _():
                for s in range(1, n_col):
                    remote(y_in.at[q, s], y_in.at[q, s], y_send.at[0], y_recv.at[q, s], (j, s)).wait_recv()
                y = y_in[q, 0]
                for s in range(1, n_col):
                    y = y + y_in[q, s]
                y_full[...] = y

            @pl.when(jnp.logical_not(near))
            def _():
                y_full[...] = y_in[q, 0]

            y = y_full[...]
            inner = lax.dot_general(y.astype(jnp.bfloat16), v_ref[q], NT, preferred_element_type=jnp.float32)
            keep = lax.broadcasted_iota(jnp.int32, (nrhs, rank_max), 1) < rank_ref[q]
            inner = jnp.where(keep, inner, 0.0).astype(jnp.bfloat16)
            p = jnp.dot(inner, u_ref[q], preferred_element_type=jnp.float32)
            for s in range(n_col):
                p_out[q, s] = p[:, s * piece:(s + 1) * piece]
            for k, peer in enumerate(peers):
                remote(p_out.at[q, peer], p_in.at[j], p_send.at[q, k], p_recv.at[j], (row, peer)).start()
            p_in[j] = p_out[q, col]

    @pl.when(feeds)
    def _():
        fold[...] = jnp.zeros_like(fold)
        for cc in range(n_col):

            @pl.when(col == cc)
            def _():
                v_copy(cc, row).wait_recv()

        for cc in range(n_col):

            @pl.when(col <= cc)
            def _():
                part = lax.dot_general(
                    inv_ref[:, cc * piece:(cc + 1) * piece],
                    v_in[cc].astype(jnp.bfloat16),
                    NT,
                    preferred_element_type=jnp.float32,
                )
                fold[...] += part

    def gather_p(j, acc):
        home = lax.rem(j, n_col)

        @pl.when(home != col)
        def _():
            remote(p_in.at[j], p_in.at[j], p_send.at[0, 0], p_recv.at[j], (row, home)).wait_recv()

        return acc - p_in[j]

    base[...] = lax.fori_loop(0, long_count, gather_p, base[...])

    @pl.when(short)
    def _():
        @pl.when(col != prev_home)
        def _():
            remote(u_in, u_in, u_send.at[0], u_recv, (row, prev_home)).wait_recv()

        u_part = u_in[...].astype(jnp.bfloat16)
        for s in range(n_col):
            remote(w_in.at[s], w_in.at[s], w_send.at[0], w_recv.at[s], (row - 1, s)).wait_recv()
        inner = w_in[0]
        for s in range(1, n_col):
            inner = inner + w_in[s]
        base[...] -= jnp.dot(inner.astype(jnp.bfloat16), u_part, preferred_element_type=jnp.float32)

    reduced = base[...].astype(jnp.bfloat16)

    @pl.when(feeds)
    def _():
        w_out[...] = jnp.dot(reduced, fold[...].astype(jnp.bfloat16), preferred_element_type=jnp.float32)
        for s in range(n_col):
            remote(w_out, w_in.at[col], w_send.at[s], w_recv.at[col], (row + 1, s)).start()

    y_row[col] = jnp.dot(reduced, inv_ref[...], preferred_element_type=jnp.float32)

    def send_y(i, carry):
        remote(y_row.at[col], y_in.at[own_slot, col], y_send.at[i], y_recv.at[own_slot, col], (i, own_home)).start()
        return carry

    lax.fori_loop(long_first, near_end, send_y, 0)
    for k, peer in enumerate(peers):
        remote(y_row.at[col], y_row.at[col], o_send.at[k], o_recv.at[col], (row, peer)).start()
    pl.when(row == 0)(log_part)
    for k, peer in enumerate(peers):
        remote(logs.at[peer], logs.at[peer], l_send.at[k], l_recv.at[peer], (row, peer)).wait_recv()
        remote(y_row.at[peer], y_row.at[peer], o_send.at[k], o_recv.at[peer], (row, peer)).wait_recv()
    y = y_row[0]
    log_sum = logs[0]
    for s in range(1, n_col):
        y = y + y_row[s]
        log_sum = log_sum + logs[s]
    y_all[...] = y

    def far_copy(i):
        return remote(y_all, y_in.at[own_slot, 0], y_send.at[i], y_recv.at[own_slot, 0], (i, col))

    def send_far(i, carry):
        far_copy(i).start()
        return carry

    lax.fori_loop(jnp.where(relays, near_end, n_row), n_row, send_far, 0)
    white_ref[0, 0] = y
    quadratic = jnp.sum(y * y, axis=1, keepdims=True) * (1.0 / width)
    lik = -0.5 * quadratic + log_sum * (1.0 / width) - 0.5 * math.log(2.0 * math.pi)
    r_id = lax.broadcasted_iota(jnp.int32, (nrhs, 128), 0)
    c_id = lax.broadcasted_iota(jnp.int32, (nrhs, 128), 1)
    flat = jnp.sum(jnp.where(r_id == c_id, lik, 0.0), axis=0, keepdims=True)
    lik_ref[0] = flat[:, :nrhs]

    def left_y(i, carry):
        remote(y_row.at[col], y_in.at[own_slot, col], y_send.at[i], y_recv.at[own_slot, col], (i, own_home)).wait_send()
        return carry

    lax.fori_loop(long_first, near_end, left_y, 0)

    def left_far(i, carry):
        far_copy(i).wait_send()
        return carry

    lax.fori_loop(jnp.where(relays, near_end, n_row), n_row, left_far, 0)
    for k, peer in enumerate(peers):
        remote(logs.at[col], logs.at[col], l_send.at[k], l_recv.at[col], (row, peer)).wait_send()
        remote(y_row.at[col], y_row.at[col], o_send.at[k], o_recv.at[col], (row, peer)).wait_send()

    @pl.when(feeds)
    def _():
        for s in range(n_col):
            remote(w_out, w_in.at[col], w_send.at[s], w_recv.at[col], (row + 1, s)).wait_send()

    @pl.when(gives)
    def _():
        for s in range(n_col):
            part = pl.ds(s, n_col - s)

            @pl.when(by_way(s))
            def _():
                remote(v_out.at[part], v_out.at[part], m_send.at[s], m_recv.at[0], (row, s)).wait_send()

            @pl.when(jnp.logical_not(by_way(s)))
            def _():
                v_copy(s, row - 1).wait_send()

        for k, peer in enumerate(peers):
            u_copy(k, peer).wait_send()

    for cc in range(n_col):
        part = pl.ds(cc, n_col - cc)

        @pl.when(by_way(col) & (col == cc))
        def _():
            remote(v_out.at[part], v_in.at[part], f_send, v_recv, (row - 1, cc)).wait_send()

    for q in range(per_col):
        j = q * n_col + col

        @pl.when(j < long_count)
        def _():
            for k, peer in enumerate(peers):
                remote(p_out.at[q, peer], p_in.at[j], p_send.at[q, k], p_recv.at[j], (row, peer)).wait_send()


def local(n_row, n_col, right_side, inverse_t, u_factor, v_factor, ranks):
    nrhs, width = right_side.shape[2:]
    per_col, _, rank_max = u_factor.shape[2:5]
    piece = width // n_col
    vmem = pl.BlockSpec(memory_space=pltpu.VMEM)
    hbm = pl.BlockSpec(memory_space=pl.ANY)
    dma = pltpu.SemaphoreType.DMA

    def f32(*shape):
        return pltpu.VMEM(shape, jnp.float32)

    def bf16(*shape):
        return pltpu.VMEM(shape, jnp.bfloat16)

    return pl.pallas_call(
        functools.partial(kernel, n_row, n_col),
        out_shape=(
            pltpu.VMEM((1, 1, nrhs, width), jnp.float32),
            pltpu.VMEM((1, 1, nrhs), jnp.float32),
        ),
        in_specs=[hbm, hbm, hbm, hbm, pl.BlockSpec(memory_space=pltpu.SMEM)],
        out_specs=(vmem, vmem),
        scratch_shapes=[
            f32(nrhs, width),
            bf16(piece, width),
            bf16(per_col, rank_max, width),
            bf16(per_col, rank_max, width),
            f32(per_col, n_col, nrhs, width),
            f32(per_col, n_col, nrhs, piece),
            f32(n_row, nrhs, piece),
            f32(n_col, nrhs, width),
            f32(n_col, 1, 128),
            f32(nrhs, piece),
            f32(n_col, rank_max, piece),
            f32(n_col, rank_max, piece),
            f32(n_col, rank_max, piece),
            f32(rank_max, piece),
            f32(piece, rank_max),
            f32(nrhs, rank_max),
            f32(n_col, nrhs, rank_max),
            f32(nrhs, width),
            f32(nrhs, width),
            dma((4,)),
            dma((n_row,)),
            dma((per_col, n_col)),
            dma((per_col, n_col)),
            dma((n_row,)),
            dma((n_col,)),
            dma((n_col,)),
            dma((n_col,)),
            dma((n_col,)),
            dma((n_col,)),
            dma,
            dma((n_col,)),
            dma,
            dma((n_col,)),
            dma((n_col,)),
            dma((n_col,)),
            dma((n_col,)),
            dma,
        ],
        compiler_params=pltpu.CompilerParams(collective_id=0, has_side_effects=True),
        name="forward_solve",
    )(right_side, inverse_t, u_factor, v_factor, ranks.reshape(per_col))


def solution(mesh):
    placed = (
        P(None, "row", None, None),
        P(None, "row", "col", None),
        P(None, "row", None, "col", None, None),
        P(None, "row", None, "col", None, None),
        P(None, "row", None, "col"),
    )
    return jax.shard_map(
        functools.partial(local, mesh.shape["row"], mesh.shape["col"]),
        mesh=mesh,
        in_specs=placed,
        out_specs=(P(None, "row", None, None), P(None, "row", None)),
        check_vma=False,
    )
```

profile of v0, /device:TPU:25, one launch (start us, length us, event | category | flops | bytes accessed | tf_op | source)
XLA Modules:
  0.0 36.9 jit_solution(16487206383531855768)
XLA Ops:
  0.6 35.1 %forward_solve.1 = (f32[1,1,4,1024]{3,2,1,0:T(4,128)S(1)}, f32[1,1,4]{2,1,0:T(1,128)S(1)}) custom-call(f32[1,1,4,1024]{3,2,1,0:T(4,128)} %rhs_hbm.1, bf16[1,1,256,1024]{3,2,1,0:T(8,128)(2,1)} %inv_hbm.1, bf16[1,1,2,1,128,1024]{5,4,3,2,1,0:T(8,128)(2,1)} %u_hbm.1, bf16[1,1,2,1,128,1024]{5,4,3,2,1,0:T(8,128)(2,1)} %v_hbm.1, s32[2]{0:T(128)} %bitcast.1), custom_call_target="tpu_custom_call" | custom-call | tf_op jit(solution)/shard_map/forward_solve/pallas_call | solution.py:389
  35.7 0.6 %copy.9 = f32[1,1,4,1024]{3,2,1,0:T(4,128)} copy(f32[1,1,4,1024]{3,2,1,0:T(4,128)S(1)} %get-tuple-element.2) | data formatting | bytes 32768
  36.4 0.5 %copy.10 = f32[1,1,4]{2,1,0:T(1,128)} copy(f32[1,1,4]{2,1,0:T(1,128)S(1)} %get-tuple-element.3) | data formatting | bytes 32
where the time goes:
time: 37.2 us; the launch traced here: 36.9 us
  Pallas kernels  35.1 us (94%)
  local copies, waits for them, and re-layouts  1.12 us (3%)
  between operations  0.64 us (2%)
    pallas_call x1, Pallas kernels, local(): pl.pallas_call(functools.partial(kernel, n_row, n_col), out_shape=(pltpu....  35.1 us
    unnamed x2, local copies, waits for them, and re-layouts  1.12 us

commit v1 on v0

--- a/solution.py
+++ b/solution.py
@@ -10,7 +10,7 @@
 
 MESH = pl.DeviceIdType.MESH
 NT = (((1,), (1,)), ((), ()))
-FIRST_SHORT = 4
+FIRST_SHORT = 3
 NEAR = 2
 
 
@@ -27,13 +27,14 @@
 
 def kernel(
     n_row, n_col,
-    rhs_hbm, inv_hbm, u_hbm, v_hbm, rank_ref,
+    rhs_hbm, inv_hbm, u_hbm, v_hbm, rank_hbm,
     white_ref, lik_ref,
     rhs_ref, inv_ref, u_ref, v_ref,
     y_in, p_out, p_in, y_row, logs, base,
     v_out, v_in, u_out, u_in, fold, w_out, w_in, y_full, y_all,
     in_sem, y_send, y_recv, p_send, p_recv, o_send, o_recv, l_send, l_recv,
-    v_send, v_recv, u_send, u_recv, w_send, w_recv, m_send, m_recv, f_send,
+    v_send, v_recv, u_send, u_recv, w_send, w_recv, m_send, m_recv, f_send, e_send,
+    rank_ref,
 ):
     row = lax.axis_index("row")
     col = lax.axis_index("col")
@@ -50,6 +51,7 @@
         pltpu.make_async_copy(u_hbm.at[0, 0, :, 0], u_ref, in_sem.at[1]),
         pltpu.make_async_copy(inv_hbm.at[0, 0], inv_ref, in_sem.at[2]),
         pltpu.make_async_copy(rhs_hbm.at[0, 0], rhs_ref, in_sem.at[3]),
+        pltpu.make_async_copy(rank_hbm, rank_ref, in_sem.at[4]),
     ]
     for copy in copies:
         copy.start()
@@ -119,6 +121,7 @@
     gives = short & (col == prev_home)
     copies[0].wait()
     copies[1].wait()
+    copies[4].wait()
 
     @pl.when(gives)
     def _():
@@ -139,20 +142,31 @@
         return remote(u_out.at[peer], u_in, u_send.at[k], u_recv, (row, peer))
 
     crosses = short & (lax.rem(row, 2) == 0)
+    half = n_col // 2
+    across = n_col - 1 - prev_home
+    split = crosses & (across < prev_home)
 
     def by_way(s):
-        return crosses & (prev_home != s) & (prev_home + s != n_col - 1)
+        return crosses & (prev_home != s) & ((across != s) | split)
+
+    def halved(s):
+        return split & (across == s)
 
     def way_copy(cc, s):
         return remote(v_out.at[cc], v_out.at[cc], m_send.at[s], m_recv.at[cc], (row, s))
 
     @pl.when(gives)
     def _():
-        for s in range(n_col):
+        for s in reversed(range(n_col)):
 
             @pl.when(by_way(s))
             def _():
-                for cc in range(s, n_col):
+                for cc in range(s, min(s + half, n_col)):
+                    way_copy(cc, s).start()
+
+            @pl.when(by_way(s) & jnp.logical_not(halved(s)))
+            def _():
+                for cc in range(s + half, n_col):
                     way_copy(cc, s).start()
 
             @pl.when(jnp.logical_not(by_way(s)))
@@ -167,10 +181,15 @@
     def _():
         def forward(cc, carry):
             remote(v_out.at[cc], v_out.at[cc], m_send.at[0], m_recv.at[cc], (row, prev_home)).wait_recv()
+
+            @pl.when(split & (across + 1 == col) & (cc >= across + half))
+            def _():
+                remote(v_out.at[cc], v_in.at[cc], e_send, v_recv, (row - 1, across)).start()
+
             remote(v_out.at[cc], v_in.at[cc], f_send, v_recv, (row - 1, col)).start()
             return carry
 
-        lax.fori_loop(col, n_col, forward, 0)
+        lax.fori_loop(col, jnp.where(halved(col), across + half, n_col), forward, 0)
 
     copies[2].wait()
     copies[3].wait()
@@ -296,12 +315,77 @@
     pl.when(row == 0)(log_part)
     for k, peer in enumerate(peers):
         remote(logs.at[peer], logs.at[peer], l_send.at[k], l_recv.at[peer], (row, peer)).wait_recv()
+    log_sum = logs[0]
+    for s in range(1, n_col):
+        log_sum = log_sum + logs[s]
+    log_part_of_lik = log_sum * (1.0 / width) - 0.5 * math.log(2.0 * math.pi)
+
+    def left_y(i, carry):
+        remote(y_row.at[col], y_in.at[own_slot, col], y_send.at[i], y_recv.at[own_slot, col], (i, own_home)).wait_send()
+        return carry
+
+    lax.fori_loop(long_first, near_end, left_y, 0)
+    for k, peer in enumerate(peers):
+        remote(logs.at[col], logs.at[col], l_send.at[k], l_recv.at[col], (row, peer)).wait_send()
+
+    @pl.when(feeds)
+    def _():
+        for s in range(n_col):
+            remote(w_out, w_in.at[col], w_send.at[s], w_recv.at[col], (row + 1, s)).wait_send()
+
+    @pl.when(gives)
+    def _():
+        for s in range(n_col):
+            part = pl.ds(s, n_col - s)
+            few = pl.ds(s, min(half, n_col - s))
+
+            @pl.when(halved(s))
+            def _():
+                remote(v_out.at[few], v_out.at[few], m_send.at[s], m_recv.at[0], (row, s)).wait_send()
+
+            @pl.when(by_way(s) & jnp.logical_not(halved(s)))
+            def _():
+                remote(v_out.at[part], v_out.at[part], m_send.at[s], m_recv.at[0], (row, s)).wait_send()
+
+            @pl.when(jnp.logical_not(by_way(s)))
+            def _():
+                v_copy(s, row - 1).wait_send()
+
+        for k, peer in enumerate(peers):
+            u_copy(k, peer).wait_send()
+
+    for cc in range(n_col):
+        part = pl.ds(cc, n_col - cc)
+        few = pl.ds(cc, min(half, n_col - cc))
+
+        @pl.when(by_way(col) & (col == cc) & jnp.logical_not(halved(cc)))
+        def _():
+            remote(v_out.at[part], v_in.at[part], f_send, v_recv, (row - 1, cc)).wait_send()
+
+        @pl.when(halved(cc) & (col == cc))
+        def _():
+            remote(v_out.at[few], v_in.at[few], f_send, v_recv, (row - 1, cc)).wait_send()
+
+        if cc + half < n_col:
+            rest = pl.ds(cc + half, n_col - cc - half)
+
+            @pl.when(split & (across == cc) & (col == cc + 1))
+            def _():
+                remote(v_out.at[rest], v_in.at[rest], e_send, v_recv, (row - 1, cc)).wait_send()
+
+    for q in range(per_col):
+        j = q * n_col + col
+
+        @pl.when(j < long_count)
+        def _():
+            for k, peer in enumerate(peers):
+                remote(p_out.at[q, peer], p_in.at[j], p_send.at[q, k], p_recv.at[j], (row, peer)).wait_send()
+
+    for k, peer in enumerate(peers):
         remote(y_row.at[peer], y_row.at[peer], o_send.at[k], o_recv.at[peer], (row, peer)).wait_recv()
     y = y_row[0]
-    log_sum = logs[0]
     for s in range(1, n_col):
         y = y + y_row[s]
-        log_sum = log_sum + logs[s]
     y_all[...] = y
 
     def far_copy(i):
@@ -314,62 +398,19 @@
     lax.fori_loop(jnp.where(relays, near_end, n_row), n_row, send_far, 0)
     white_ref[0, 0] = y
     quadratic = jnp.sum(y * y, axis=1, keepdims=True) * (1.0 / width)
-    lik = -0.5 * quadratic + log_sum * (1.0 / width) - 0.5 * math.log(2.0 * math.pi)
+    lik = -0.5 * quadratic + log_part_of_lik
     r_id = lax.broadcasted_iota(jnp.int32, (nrhs, 128), 0)
     c_id = lax.broadcasted_iota(jnp.int32, (nrhs, 128), 1)
     flat = jnp.sum(jnp.where(r_id == c_id, lik, 0.0), axis=0, keepdims=True)
     lik_ref[0] = flat[:, :nrhs]
 
-    def left_y(i, carry):
-        remote(y_row.at[col], y_in.at[own_slot, col], y_send.at[i], y_recv.at[own_slot, col], (i, own_home)).wait_send()
-        return carry
-
-    lax.fori_loop(long_first, near_end, left_y, 0)
-
     def left_far(i, carry):
         far_copy(i).wait_send()
         return carry
 
     lax.fori_loop(jnp.where(relays, near_end, n_row), n_row, left_far, 0)
     for k, peer in enumerate(peers):
-        remote(logs.at[col], logs.at[col], l_send.at[k], l_recv.at[col], (row, peer)).wait_send()
         remote(y_row.at[col], y_row.at[col], o_send.at[k], o_recv.at[col], (row, peer)).wait_send()
-
-    @pl.when(feeds)
-    def _():
-        for s in range(n_col):
-            remote(w_out, w_in.at[col], w_send.at[s], w_recv.at[col], (row + 1, s)).wait_send()
-
-    @pl.when(gives)
-    def _():
-        for s in range(n_col):
-            part = pl.ds(s, n_col - s)
-
-            @pl.when(by_way(s))
-            def _():
-                remote(v_out.at[part], v_out.at[part], m_send.at[s], m_recv.at[0], (row, s)).wait_send()
-
-            @pl.when(jnp.logical_not(by_way(s)))
-            def _():
-                v_copy(s, row - 1).wait_send()
-
-        for k, peer in enumerate(peers):
-            u_copy(k, peer).wait_send()
-
-    for cc in range(n_col):
-        part = pl.ds(cc, n_col - cc)
-
-        @pl.when(by_way(col) & (col == cc))
-        def _():
-            remote(v_out.at[part], v_in.at[part], f_send, v_recv, (row - 1, cc)).wait_send()
-
-    for q in range(per_col):
-        j = q * n_col + col
-
-        @pl.when(j < long_count)
-        def _():
-            for k, peer in enumerate(peers):
-                remote(p_out.at[q, peer], p_in.at[j], p_send.at[q, k], p_recv.at[j], (row, peer)).wait_send()
 
 
 def local(n_row, n_col, right_side, inverse_t, u_factor, v_factor, ranks):
@@ -392,7 +433,7 @@
             pltpu.VMEM((1, 1, nrhs, width), jnp.float32),
             pltpu.VMEM((1, 1, nrhs), jnp.float32),
         ),
-        in_specs=[hbm, hbm, hbm, hbm, pl.BlockSpec(memory_space=pltpu.SMEM)],
+        in_specs=[hbm, hbm, hbm, hbm, hbm],
         out_specs=(vmem, vmem),
         scratch_shapes=[
             f32(nrhs, width),
@@ -414,7 +455,7 @@
             f32(n_col, nrhs, rank_max),
             f32(nrhs, width),
             f32(nrhs, width),
-            dma((4,)),
+            dma((5,)),
             dma((n_row,)),
             dma((per_col, n_col)),
             dma((per_col, n_col)),
@@ -432,6 +473,8 @@
             dma((n_col,)),
             dma((n_col,)),
             dma,
+            dma,
+            pltpu.SMEM((per_col,), jnp.int32),
         ],
         compiler_params=pltpu.CompilerParams(collective_id=0, has_side_effects=True),
         name="forward_solve",

time: 37.2 us -> 35 us (0.941)
  Pallas kernels: 35.1 us -> 33.1 us
    pallas_call x1, Pallas kernels: 35.1 us -> 33.1 us  [local(): pl.pallas_call(functools.partial(kernel, n_row, n_col), out_shape=(pltpu....]
where the time goes in v1:
time: 35 us; the launch traced here: 34.9 us
  Pallas kernels  33.1 us (95%)
  local copies, waits for them, and re-layouts  1.12 us (3%)
  between operations  0.64 us (2%)
    pallas_call x1, Pallas kernels, local(): pl.pallas_call(functools.partial(kernel, n_row, n_col), out_shape=(pltpu....  33.1 us
    unnamed x2, local copies, waits for them, and re-layouts  1.12 us

profile of v1, /device:TPU:25, one launch (start us, length us, event | category | flops | bytes accessed | tf_op | source)
XLA Modules:
  0.0 34.9 jit_solution(15114375440706537589)
XLA Ops:
  0.6 33.1 %forward_solve.1 = (f32[1,1,4,1024]{3,2,1,0:T(4,128)S(1)}, f32[1,1,4]{2,1,0:T(1,128)S(1)}) custom-call(f32[1,1,4,1024]{3,2,1,0:T(4,128)} %rhs_hbm.1, bf16[1,1,256,1024]{3,2,1,0:T(8,128)(2,1)} %inv_hbm.1, bf16[1,1,2,1,128,1024]{5,4,3,2,1,0:T(8,128)(2,1)} %u_hbm.1, bf16[1,1,2,1,128,1024]{5,4,3,2,1,0:T(8,128)(2,1)} %v_hbm.1, s32[2]{0:T(128)} %bitcast.1), custom_call_target="tpu_custom_call" | custom-call | tf_op jit(solution)/shard_map/forward_solve/pallas_call | solution.py:430
  33.8 0.6 %copy.9 = f32[1,1,4,1024]{3,2,1,0:T(4,128)} copy(f32[1,1,4,1024]{3,2,1,0:T(4,128)S(1)} %get-tuple-element.2) | data formatting | bytes 32768
  34.4 0.5 %copy.10 = f32[1,1,4]{2,1,0:T(1,128)} copy(f32[1,1,4]{2,1,0:T(1,128)S(1)} %get-tuple-element.3) | data formatting | bytes 32

commit v2 on v1

v2 whole, which is shorter than its diff:
```python
import functools
import math

import jax
import jax.numpy as jnp
from jax import lax
from jax.experimental import pallas as pl
from jax.experimental.pallas import tpu as pltpu
from jax.sharding import PartitionSpec as P

MESH = pl.DeviceIdType.MESH
NT = (((1,), (1,)), ((), ()))
FIRST_SHORT = 3
NEAR = 3


def remote(src, dst, send_sem, recv_sem, device):
    return pltpu.make_async_remote_copy(
        src_ref=src,
        dst_ref=dst,
        send_sem=send_sem,
        recv_sem=recv_sem,
        device_id=device,
        device_id_type=MESH,
    )


def kernel(
    n_row, n_col,
    rhs_hbm, inv_hbm, u_hbm, v_hbm, rank_hbm,
    white_ref, lik_ref,
    rhs_ref, inv_ref, u_ref, v_ref, rank_ref,
    y_in, p_out, p_in, y_row, logs, base, y_full, y_all,
    v_out, v_in, u_out, u_in, fold, w_out, w_in,
    x_out, x_in, t_out, t_in, fold_x, wx_out, wx_in,
    d_out, d_in, d_tile, du_out, du_in, du_tile, pd_out, l_out, l_in, wl_out, wl_in, we_in,
    a_out, a_in, a_sum,
    in_sem, y_send, y_recv, p_send, p_recv, o_send, o_recv, l_send, l_recv,
    v_send, v_recv, u_send, u_recv, w_send, w_recv, m_recv, f_send, e_send, ready,
    x_recv, t_recv, k_recv, d_send, d_recv, du_send, du_recv, pd_send, wl_send, wl_recv, wp_send,
    we_send, we_recv, wx_send, wx_recv, a_send, a_recv,
):
    row = lax.axis_index("row")
    col = lax.axis_index("col")
    per_col, rank_max, width = u_ref.shape
    nrhs = rhs_ref.shape[0]
    piece = width // n_col
    half = n_col // 2
    peers = [lax.rem(col + k, n_col) for k in range(1, n_col)]
    others = pl.ds(0, n_col - 1)
    own_slot = row // n_col
    own_home = lax.rem(row, n_col)
    end = n_row - 1
    even_end = n_row - 2
    ahead = n_row - 3

    def longs_of(i):
        count = jnp.where(i >= FIRST_SHORT, i - 1, i)
        handed = (lax.rem(i, 2) == 0) & (i >= 2)
        return count - jnp.where(handed, 1, 0) - jnp.where(i >= even_end, 1, 0)

    def near_of(i):
        return NEAR + jnp.where(i >= 2, 1, 0)

    copies = [
        pltpu.make_async_copy(v_hbm.at[0, 0, :, 0], v_ref, in_sem.at[0]),
        pltpu.make_async_copy(u_hbm.at[0, 0, :, 0], u_ref, in_sem.at[1]),
        pltpu.make_async_copy(inv_hbm.at[0, 0], inv_ref, in_sem.at[2]),
        pltpu.make_async_copy(rhs_hbm.at[0, 0], rhs_ref, in_sem.at[3]),
        pltpu.make_async_copy(rank_hbm, rank_ref, in_sem.at[4]),
    ]
    for copy in copies:
        copy.start()

    even = lax.rem(row, 2) == 0
    short = row >= FIRST_SHORT
    feeds = (row + 1 >= FIRST_SHORT) & (row < end)
    is_end = row == end
    is_even_end = row == even_end
    is_ahead = row == ahead
    long_count = longs_of(row)
    near_end = jnp.minimum(row + near_of(row) + 1, n_row)
    relays = col == own_home

    barrier = pltpu.get_barrier_semaphore()

    def signal(sem, i, s):
        pl.semaphore_signal(sem, inc=1, device_id=(i, s), device_id_type=MESH)

    def row_of(i, cond, act):
        @pl.when(cond)
        def _():
            for s in range(n_col):
                act(i, s)

        return jnp.where(cond, n_col, 0)

    def above(act):
        yield row + 1, row_of(row + 1, row < end, act)
        for d in range(2, NEAR + 2):
            wide = is_ahead if d == 2 else jnp.bool_(False)
            one = (row + d < n_row) & (d <= near_of(row)) & jnp.logical_not(wide)

            @pl.when(one)
            def _():
                act(row + d, own_home)

            yield row + d, jnp.where(one, 1, 0)
            if d == 2:
                yield row + d, row_of(row + d, wide, act)

    def below(act):
        row_of(row - 1, row > 0, act)
        count = jnp.where(row > 0, n_col, 0)
        for d in range(2, NEAR + 2):
            fed = (row >= d) & (d <= near_of(row - d)) & (lax.rem(jnp.maximum(row - d, 0), n_col) == col)
            if d == 2:
                fed = fed | is_end
            count += row_of(row - d, fed, act)
        for q in range(per_col):
            j = q * n_col + col
            far = j < row - near_of(j)

            @pl.when(far)
            def _():
                act(j, col)

            count += jnp.where(far, 1, 0)
        return count

    def at_once(low, high):
        return (low == 0) & (high <= NEAR)

    for peer in peers:
        signal(barrier, row, peer)
    greeted = jnp.int32(n_col - 1)
    answers = jnp.int32(0)
    for i, count in above(lambda i, s: signal(barrier, i, s)):
        quick = at_once(row, i)
        greeted += jnp.where(quick, count, 0)
        answers += jnp.where(quick, 0, count)

    def greet_far(i, count):
        signal(barrier, i, col)
        return count + 1

    answers = lax.fori_loop(jnp.where(relays, near_end, n_row), n_row, greet_far, answers)

    def greet_quick(i, s):
        @pl.when(at_once(i, row))
        def _():
            signal(barrier, i, s)

    def answer(i, s):
        @pl.when(jnp.logical_not(at_once(i, row)))
        def _():
            signal(ready, i, s)

    greeted += below(greet_quick)

    prev = jnp.maximum(row - 1, 0)
    prev_slot = prev // n_col
    prev_home = lax.rem(prev, n_col)
    gives = short & (col == prev_home)
    crosses = short & even
    far_slot = ahead // n_col
    far_home = ahead % n_col
    gives_far = is_end & (col == far_home)
    handed = even & (row >= 2)
    mine = jnp.where(handed, long_count + jnp.where(is_even_end, 1, 0), 0)
    mine_slot = mine // n_col
    mine_home = lax.rem(mine, n_col)
    hands = handed & (col == mine_home)
    taken = (row >= 3) & jnp.logical_not(even)
    theirs = jnp.where(taken, longs_of(prev) + jnp.where(is_end, 1, 0), 0)
    their_home = lax.rem(theirs, n_col)
    takes = taken & (col == their_home)
    whole = even_end - 3
    whole_slot = whole // n_col
    whole_home = whole % n_col
    hands_whole = is_even_end & (col == whole_home)
    takes_whole = is_end & (col == whole_home)

    def masked_u(slot):
        keep = lax.broadcasted_iota(jnp.int32, (rank_max, width), 0) < rank_ref[slot]
        return jnp.where(keep, u_ref[slot].astype(jnp.float32), 0.0)

    def cut(tile, into):
        for s in range(n_col):
            into[s] = tile[:, s * piece:(s + 1) * piece]

    copies[0].wait()
    copies[1].wait()
    copies[4].wait()

    @pl.when(hands)
    def _():
        d_out[...] = v_ref[mine_slot].astype(jnp.float32)
        cut(masked_u(mine_slot), l_out)

    @pl.when(hands_whole)
    def _():
        d_out[...] = v_ref[whole_slot].astype(jnp.float32)
        du_out[...] = masked_u(whole_slot)

    @pl.when(gives)
    def _():
        cut(v_ref[prev_slot].astype(jnp.float32), v_out)
        cut(masked_u(prev_slot), u_out)

    @pl.when(gives_far)
    def _():
        cut(v_ref[far_slot].astype(jnp.float32), x_out)
        cut(masked_u(far_slot), t_out)

    pl.semaphore_wait(barrier, greeted)
    below(answer)

    def by_way(home, s, cc):
        across = n_col - 1 - home
        return (home != s) & jnp.where(across < home, (across != s) | (cc < s + half), (s > home) | (cc < s + half))

    def is_late(home, s, cc):
        across = n_col - 1 - home
        return (across == s) & (across < home) & (cc >= s + half)

    def joined(home, s):
        across = n_col - 1 - home
        return (across > home) & (across == s)

    def spread(out, into, recv, target, home, cross):
        for s in reversed(range(n_col)):
            if s > 0:

                @pl.when(cross & joined(home, s - 1))
                def _():
                    remote(out.at[s - 1], out.at[s - 1], v_send.at[s], m_recv.at[s - 1], (row, s)).start()

            for cc in range(s, n_col):
                gone = cross & joined(home, s)
                way = cross & by_way(home, s, cc)
                later = cross & is_late(home, s, cc)

                @pl.when(way & jnp.logical_not(gone))
                def _():
                    remote(out.at[cc], out.at[cc], v_send.at[s], m_recv.at[cc], (row, s)).start()

                @pl.when(jnp.logical_not(way | later | gone))
                def _():
                    remote(out.at[cc], into.at[cc], v_send.at[s], recv, (target, s)).start()

    def spread_late(out, into, recv, target, home):
        for s in range(n_col):
            for cc in range(min(s + half, n_col), n_col):

                @pl.when(is_late(home, s, cc))
                def _():
                    remote(out.at[cc], into.at[cc], v_send.at[s], recv, (target, s)).start()

    def spread_done(out, home, cross):
        for s in range(n_col):
            part = pl.ds(s, n_col - s)
            gone = cross & joined(home, s)
            more = (cross & joined(home, s - 1)) if s > 0 else jnp.bool_(False)

            @pl.when(jnp.logical_not(gone | more))
            def _():
                remote(out.at[part], out.at[part], v_send.at[s], m_recv.at[0], (row, s)).wait_send()

            if s > 0:
                part_more = pl.ds(s - 1, n_col - s + 1)

                @pl.when(more)
                def _():
                    remote(out.at[part_more], out.at[part_more], v_send.at[s], m_recv.at[0], (row, s)).wait_send()

    def relay(out, into, recv, target, home):
        across = n_col - 1 - home
        more = joined(home, col - 1)
        first = jnp.where(more, col - 1, col)
        part = jnp.where(across < home, across == col, col < home)
        stop = jnp.where(joined(home, col), col, jnp.where(part, jnp.minimum(col + half, n_col), n_col))

        def forward(cc, carry):
            remote(out.at[cc], out.at[cc], v_send.at[0], m_recv.at[cc], (row, home)).wait_recv()

            @pl.when(cc >= col)
            def _():
                remote(out.at[cc], into.at[cc], f_send, recv, (target, col)).start()

            @pl.when(more)
            def _():
                remote(out.at[cc], into.at[cc], e_send, recv, (target, across)).start()

            return carry

        lax.fori_loop(first, stop, forward, 0)

    def relay_done(out, home):
        across = n_col - 1 - home
        for cc in range(n_col):
            few = pl.ds(cc, min(half, n_col - cc))
            here = (col == cc) & jnp.logical_not(joined(home, cc))
            half_way = jnp.where(across < home, across == cc, cc < home)

            @pl.when(here & jnp.logical_not(half_way))
            def _():
                part = pl.ds(cc, n_col - cc)
                remote(out.at[part], out.at[part], f_send, v_recv, (row, home)).wait_send()

            @pl.when(here & half_way)
            def _():
                remote(out.at[few], out.at[few], f_send, v_recv, (row, home)).wait_send()

            if cc > 0:

                @pl.when((col == cc) & joined(home, cc - 1))
                def _():
                    part = pl.ds(cc - 1, n_col - cc + 1)
                    remote(out.at[part], out.at[part], e_send, v_recv, (row, home)).wait_send()

    def share(out, into, recv):
        for peer in peers:
            remote(out.at[peer], into, u_send, recv, (row, peer)).start()
        into[...] = out[col]

    def share_done(out):
        remote(out.at[others], out.at[others], u_send, u_recv, (row, peers[0])).wait_send()

    def shared_wait(into, recv, home):
        @pl.when(col != home)
        def _():
            remote(into, into, u_send, recv, (row, home)).wait_recv()

    @pl.when(hands)
    def _():
        share(l_out, l_in, k_recv)

    @pl.when(gives & is_even_end)
    def _():
        share(u_out, u_in, u_recv)

    @pl.when(gives)
    def _():
        spread(v_out, v_in, v_recv, row - 1, prev_home, crosses)

    @pl.when(gives_far)
    def _():
        spread(x_out, x_in, x_recv, row - 2, far_home, jnp.bool_(True))

    @pl.when((handed) & (answers > 0))
    def _():
        pl.semaphore_wait(ready, answers)

    @pl.when(hands | hands_whole)
    def _():
        remote(d_out, d_in, d_send, d_recv, (row + 1, col)).start()

    @pl.when(hands_whole)
    def _():
        remote(du_out, du_in, du_send, du_recv, (row + 1, col)).start()

    @pl.when(crosses & (col != prev_home))
    def _():
        relay(v_out, v_in, v_recv, row - 1, prev_home)

    copies[2].wait()
    copies[3].wait()

    for cc in range(n_col):

        @pl.when(col == cc)
        def _():
            base[...] = rhs_ref[:, cc * piece:(cc + 1) * piece]

    def log_part():
        for cc in range(n_col):

            @pl.when(col == cc)
            def _():
                block = inv_ref[:, cc * piece:(cc + 1) * piece].astype(jnp.float32)
                r_id = lax.broadcasted_iota(jnp.int32, (piece, piece), 0)
                c_id = lax.broadcasted_iota(jnp.int32, (piece, piece), 1)
                diagonal = jnp.sum(jnp.where(r_id == c_id, block, 0.0), axis=0, keepdims=True)
                total = jnp.sum(jnp.log(diagonal), axis=1, keepdims=True)
                logs[cc] = jnp.broadcast_to(total, (1, 128))

        for peer in peers:
            remote(logs.at[col], logs.at[col], l_send, l_recv, (row, peer)).start()

    pl.when(row > 0)(log_part)

    @pl.when(gives & jnp.logical_not(even))
    def _():
        spread_done(v_out, prev_home, crosses)
        share(u_out, u_in, u_recv)

    def fold_with(into, recv, target):
        target[...] = jnp.zeros_like(target)
        for cc in range(n_col):
            part = pl.ds(cc, n_col - cc)

            @pl.when(col == cc)
            def _():
                remote(into.at[part], into.at[part], f_send, recv, (row, cc)).wait_recv()

        for cc in range(n_col):

            @pl.when(col <= cc)
            def _():
                target[...] += lax.dot_general(
                    inv_ref[:, cc * piece:(cc + 1) * piece],
                    into[cc].astype(jnp.bfloat16),
                    NT,
                    preferred_element_type=jnp.float32,
                )

    def long_step(q, cond):
        j = q * n_col + col

        @pl.when((j < long_count) & cond)
        def _():
            near = row - j <= near_of(j)

            @pl.when(near)
            def _():
                remote(y_in.at[q], y_in.at[q], y_send.at[0], y_recv.at[q], (j, col)).wait_recv()
                y = y_in[q, 0]
                for s in range(1, n_col):
                    y = y + y_in[q, s]
                y_full[...] = y

            @pl.when(jnp.logical_not(near))
            def _():
                remote(y_in.at[q, 0], y_in.at[q, 0], y_send.at[0], y_recv.at[q], (j, col)).wait_recv()
                y_full[...] = y_in[q, 0]

            y = y_full[...].astype(jnp.bfloat16)

            @pl.when(takes & (j == theirs))
            def _():
                wl_out[...] = lax.dot_general(y, d_tile[...], NT, preferred_element_type=jnp.float32)
                for s in range(n_col):
                    remote(wl_out, wl_in, wl_send, wl_recv, (row - 1, s)).start()

                @pl.when(is_end)
                def _():
                    for peer in peers:
                        remote(wl_out, wl_in, wp_send, wl_recv, (row, peer)).start()
                    wl_in[...] = wl_out[...]

            @pl.when(takes_whole & (j == whole))
            def _():
                inner = lax.dot_general(y, d_tile[...], NT, preferred_element_type=jnp.float32)
                p = jnp.dot(inner.astype(jnp.bfloat16), du_tile[...], preferred_element_type=jnp.float32)
                for s in range(n_col):
                    pd_out[s] = p[:, s * piece:(s + 1) * piece]
                    remote(pd_out.at[s], p_in.at[j], pd_send, p_recv.at[j], (row - 1, s)).start()

            inner = lax.dot_general(y, v_ref[q], NT, preferred_element_type=jnp.float32)
            keep = lax.broadcasted_iota(jnp.int32, (nrhs, rank_max), 1) < rank_ref[q]
            inner = jnp.where(keep, inner, 0.0).astype(jnp.bfloat16)
            p = jnp.dot(inner, u_ref[q], preferred_element_type=jnp.float32)
            for s in range(n_col):
                p_out[q, s] = p[:, s * piece:(s + 1) * piece]
            for peer in peers:
                remote(p_out.at[q, peer], p_in.at[j], p_send.at[q], p_recv.at[j], (row, peer)).start()
            p_in[j] = p_out[q, col]

    for q in range(per_col):
        long_step(q, is_even_end & (q * n_col + col <= row - 5))

    @pl.when(is_even_end)
    def _():
        fold_with(v_in, v_recv, fold)
        factor = fold[...].astype(jnp.bfloat16)
        shared_wait(u_in, u_recv, prev_home)
        shared_wait(l_in, k_recv, mine_home)
        a_out[0] = jnp.dot(u_in[...].astype(jnp.bfloat16), factor, preferred_element_type=jnp.float32)
        a_out[1] = jnp.dot(l_in[...].astype(jnp.bfloat16), factor, preferred_element_type=jnp.float32)
        for k in range(2):
            for s in range(n_col):
                remote(a_out.at[k], a_in.at[k, col], a_send, a_recv, (row + 1, s)).start()

    @pl.when(takes | takes_whole)
    def _():
        remote(d_in, d_in, d_send, d_recv, (row - 1, col)).wait_recv()
        d_tile[...] = d_in[...].astype(jnp.bfloat16)

    @pl.when(takes_whole)
    def _():
        remote(du_in, du_in, du_send, du_recv, (row - 1, col)).wait_recv()
        du_tile[...] = du_in[...].astype(jnp.bfloat16)

    @pl.when(is_end & (col != far_home))
    def _():
        relay(x_out, x_in, x_recv, row - 2, far_home)

    for q in range(per_col):
        long_step(q, jnp.logical_not(is_even_end & (q * n_col + col <= row - 5)))

    @pl.when(feeds & jnp.logical_not(is_even_end))
    def _():
        fold_with(v_in, v_recv, fold)

    @pl.when(gives & crosses)
    def _():
        spread_late(v_out, v_in, v_recv, row - 1, prev_home)

    @pl.when(gives & crosses & jnp.logical_not(is_even_end))
    def _():
        share(u_out, u_in, u_recv)

    @pl.when(gives_far)
    def _():
        spread_late(x_out, x_in, x_recv, row - 2, far_home)
        share(t_out, t_in, t_recv)

    @pl.when(is_ahead)
    def _():
        fold_with(x_in, x_recv, fold_x)

    @pl.when(is_end)
    def _():
        remote(a_in, a_in, a_send, a_recv, (row - 1, 0)).wait_recv()
        for k in range(2):
            total = a_in[k, 0]
            for s in range(1, n_col):
                total = total + a_in[k, s]
            a_sum[k] = total.astype(jnp.bfloat16)

    def gather_p(j, acc):
        home = lax.rem(j, n_col)

        @pl.when(home != col)
        def _():
            remote(p_in.at[j], p_in.at[j], p_send.at[0], p_recv.at[j], (row, home)).wait_recv()

        return acc - p_in[j]

    base[...] = lax.fori_loop(0, long_count, gather_p, base[...])

    @pl.when(is_even_end)
    def _():
        remote(p_in.at[whole], p_in.at[whole], p_send.at[0], p_recv.at[whole], (row + 1, whole_home)).wait_recv()
        base[...] -= p_in[whole]

    def send_w(out, into, send, recv, i):
        for s in range(n_col):
            remote(out, into.at[col], send, recv, (i, s)).start()

    def wait_w(into, send, recv, i):
        remote(into, into, send, recv, (i, 0)).wait_recv()
        total = into[0]
        for s in range(1, n_col):
            total = total + into[s]
        return total

    @pl.when(is_even_end)
    def _():
        w_out[...] = jnp.dot(base[...].astype(jnp.bfloat16), fold[...].astype(jnp.bfloat16), preferred_element_type=jnp.float32)
        send_w(w_out, w_in, w_send, w_recv, row + 1)

    @pl.when(handed)
    def _():
        @pl.when(jnp.logical_not(is_even_end))
        def _():
            shared_wait(l_in, k_recv, mine_home)

        l_part = l_in[...].astype(jnp.bfloat16)
        remote(wl_in, wl_in, wl_send, wl_recv, (row + 1, mine_home)).wait_recv()
        base[...] -= jnp.dot(wl_in[...].astype(jnp.bfloat16), l_part, preferred_element_type=jnp.float32)

    @pl.when(short & jnp.logical_not(is_end))
    def _():
        @pl.when(jnp.logical_not(is_even_end))
        def _():
            shared_wait(u_in, u_recv, prev_home)

        u_part = u_in[...].astype(jnp.bfloat16)
        inner = wait_w(w_in, w_send, w_recv, row - 1)
        base[...] -= jnp.dot(inner.astype(jnp.bfloat16), u_part, preferred_element_type=jnp.float32)

    @pl.when(is_end)
    def _():
        shared_wait(u_in, u_recv, prev_home)
        shared_wait(t_in, t_recv, far_home)
        u_part = u_in[...].astype(jnp.bfloat16)
        t_part = t_in[...].astype(jnp.bfloat16)

        @pl.when(jnp.logical_not(takes))
        def _():
            remote(wl_in, wl_in, wp_send, wl_recv, (row, their_home)).wait_recv()

        inner = wait_w(w_in, w_send, w_recv, row - 1)
        inner -= jnp.dot(wl_in[...].astype(jnp.bfloat16), a_sum[1], preferred_element_type=jnp.float32)
        late = wait_w(wx_in, wx_send, wx_recv, row - 2)
        base[...] -= jnp.dot(late.astype(jnp.bfloat16), t_part, preferred_element_type=jnp.float32)
        late = wait_w(we_in, we_send, we_recv, row - 2)
        inner -= jnp.dot(late.astype(jnp.bfloat16), a_sum[0], preferred_element_type=jnp.float32)
        base[...] -= jnp.dot(inner.astype(jnp.bfloat16), u_part, preferred_element_type=jnp.float32)

    reduced = base[...].astype(jnp.bfloat16)

    @pl.when((jnp.logical_not(even)) & (answers > 0))
    def _():
        pl.semaphore_wait(ready, answers)

    @pl.when(feeds & jnp.logical_not(is_even_end))
    def _():
        w_out[...] = jnp.dot(reduced, fold[...].astype(jnp.bfloat16), preferred_element_type=jnp.float32)

        @pl.when(is_ahead)
        def _():
            send_w(w_out, we_in, we_send, we_recv, row + 2)
            wx_out[...] = jnp.dot(reduced, fold_x[...].astype(jnp.bfloat16), preferred_element_type=jnp.float32)
            send_w(wx_out, wx_in, wx_send, wx_recv, row + 2)

        send_w(w_out, w_in, w_send, w_recv, row + 1)

    y_row[col] = jnp.dot(reduced, inv_ref[...], preferred_element_type=jnp.float32)

    def near_copy(i):
        return remote(y_row.at[col], y_in.at[own_slot, col], y_send.at[i], y_recv.at[own_slot], (i, own_home))

    def send_y(i, carry):
        @pl.when(row < longs_of(i))
        def _():
            near_copy(i).start()

        return carry

    lax.fori_loop(row + 1, near_end, send_y, 0)
    for peer in peers:
        remote(y_row.at[col], y_row.at[col], o_send, o_recv, (row, peer)).start()
    pl.when(row == 0)(log_part)

    remote(logs.at[others], logs.at[others], l_send, l_recv, (row, peers[0])).wait()
    log_sum = logs[0]
    for s in range(1, n_col):
        log_sum = log_sum + logs[s]
    log_term = log_sum * (1.0 / width) - 0.5 * math.log(2.0 * math.pi)

    def left_y(i, carry):
        @pl.when(row < longs_of(i))
        def _():
            near_copy(i).wait_send()

        return carry

    lax.fori_loop(row + 1, near_end, left_y, 0)

    @pl.when(feeds)
    def _():
        remote(w_in, w_in, w_send, w_recv, (row + 1, 0)).wait_send()

    @pl.when(is_ahead)
    def _():
        remote(w_in, w_in, we_send, we_recv, (row + 2, 0)).wait_send()
        remote(w_in, w_in, wx_send, wx_recv, (row + 2, 0)).wait_send()

    @pl.when(is_even_end)
    def _():
        remote(a_in, a_in, a_send, a_recv, (row + 1, 0)).wait_send()

    @pl.when(takes)
    def _():
        remote(w_in, w_in, wl_send, wl_recv, (row - 1, 0)).wait_send()

        @pl.when(is_end)
        def _():
            remote(w_in.at[others], w_in.at[others], wp_send, wl_recv, (row, peers[0])).wait_send()

    @pl.when(hands)
    def _():
        remote(d_out, d_in, d_send, d_recv, (row + 1, col)).wait_send()
        share_done(l_out)

    @pl.when(hands_whole)
    def _():
        remote(d_out, d_in, d_send, d_recv, (row + 1, col)).wait_send()
        remote(du_out, du_in, du_send, du_recv, (row + 1, col)).wait_send()

    @pl.when(takes_whole)
    def _():
        remote(pd_out, pd_out, pd_send, p_recv.at[0], (row - 1, 0)).wait_send()

    @pl.when(gives & even)
    def _():
        spread_done(v_out, prev_home, crosses)

    @pl.when(gives)
    def _():
        share_done(u_out)

    @pl.when(gives_far)
    def _():
        spread_done(x_out, far_home, jnp.bool_(True))
        share_done(t_out)

    @pl.when(crosses & (col != prev_home))
    def _():
        relay_done(v_out, prev_home)

    @pl.when(is_end & (col != far_home))
    def _():
        relay_done(x_out, far_home)

    for q in range(per_col):

        @pl.when(q * n_col + col < long_count)
        def _():
            part = p_out.at[q, others]
            remote(part, part, p_send.at[q], p_recv.at[0], (row, peers[0])).wait_send()

    remote(y_row.at[others], y_row.at[others], o_send, o_recv, (row, peers[0])).wait_recv()
    y = y_row[0]
    for s in range(1, n_col):
        y = y + y_row[s]
    y_all[...] = y

    def far_copy(i):
        return remote(y_all, y_in.at[own_slot, 0], y_send.at[i], y_recv.at[own_slot], (i, col))

    def send_far(i, carry):
        far_copy(i).start()
        return carry

    @pl.when((row == 0) & (answers > 0))
    def _():
        pl.semaphore_wait(ready, answers)

    lax.fori_loop(jnp.where(relays, near_end, n_row), n_row, send_far, 0)
    white_ref[0, 0] = y
    quadratic = jnp.sum(y * y, axis=1, keepdims=True) * (1.0 / width)
    lik = -0.5 * quadratic + log_term
    r_id = lax.broadcasted_iota(jnp.int32, (nrhs, 128), 0)
    c_id = lax.broadcasted_iota(jnp.int32, (nrhs, 128), 1)
    flat = jnp.sum(jnp.where(r_id == c_id, lik, 0.0), axis=0, keepdims=True)
    lik_ref[0] = flat[:, :nrhs]

    def left_far(i, carry):
        far_copy(i).wait_send()
        return carry

    lax.fori_loop(jnp.where(relays, near_end, n_row), n_row, left_far, 0)
    remote(y_row.at[others], y_row.at[others], o_send, o_recv, (row, peers[0])).wait_send()


def local(n_row, n_col, right_side, inverse_t, u_factor, v_factor, ranks):
    nrhs, width = right_side.shape[2:]
    per_col, _, rank_max = u_factor.shape[2:5]
    piece = width // n_col
    vmem = pl.BlockSpec(memory_space=pltpu.VMEM)
    hbm = pl.BlockSpec(memory_space=pl.ANY)
    dma = pltpu.SemaphoreType.DMA

    def f32(*shape):
        return pltpu.VMEM(shape, jnp.float32)

    def bf16(*shape):
        return pltpu.VMEM(shape, jnp.bfloat16)

    tile_set = [
        f32(n_col, rank_max, piece),
        f32(n_col, rank_max, piece),
        f32(n_col, rank_max, piece),
        f32(rank_max, piece),
        f32(piece, rank_max),
        f32(nrhs, rank_max),
        f32(n_col, nrhs, rank_max),
    ]
    return pl.pallas_call(
        functools.partial(kernel, n_row, n_col),
        out_shape=(
            pltpu.VMEM((1, 1, nrhs, width), jnp.float32),
            pltpu.VMEM((1, 1, nrhs), jnp.float32),
        ),
        in_specs=[hbm, hbm, hbm, hbm, hbm],
        out_specs=(vmem, vmem),
        scratch_shapes=[
            f32(nrhs, width),
            bf16(piece, width),
            bf16(per_col, rank_max, width),
            bf16(per_col, rank_max, width),
            pltpu.SMEM((per_col,), jnp.int32),
            f32(per_col, n_col, nrhs, width),
            f32(per_col, n_col, nrhs, piece),
            f32(n_row, nrhs, piece),
            f32(n_col, nrhs, width),
            f32(n_col, 1, 128),
            f32(nrhs, piece),
            f32(nrhs, width),
            f32(nrhs, width),
            *tile_set,
            *tile_set,
            f32(rank_max, width),
            f32(rank_max, width),
            bf16(rank_max, width),
            f32(rank_max, width),
            f32(rank_max, width),
            bf16(rank_max, width),
            f32(n_col, nrhs, piece),
            f32(n_col, rank_max, piece),
            f32(rank_max, piece),
            f32(nrhs, rank_max),
            f32(nrhs, rank_max),
            f32(n_col, nrhs, rank_max),
            f32(2, rank_max, rank_max),
            f32(2, n_col, rank_max, rank_max),
            bf16(2, rank_max, rank_max),
            dma((5,)),
            dma((n_row,)),
            dma((per_col,)),
            dma((per_col,)),
            dma((n_row,)),
            dma, dma, dma, dma,
            dma((n_col,)),
            dma, dma, dma, dma, dma,
            dma((n_col,)),
            dma, dma,
            pltpu.SemaphoreType.REGULAR,
            dma, dma, dma, dma, dma, dma, dma, dma,
            dma, dma, dma,
            dma, dma, dma, dma, dma, dma,
        ],
        compiler_params=pltpu.CompilerParams(collective_id=0, has_side_effects=True),
        name="forward_solve",
    )(right_side, inverse_t, u_factor, v_factor, ranks.reshape(per_col))


def solution(mesh):
    placed = (
        P(None, "row", None, None),
        P(None, "row", "col", None),
        P(None, "row", None, "col", None, None),
        P(None, "row", None, "col", None, None),
        P(None, "row", None, "col"),
    )
    return jax.shard_map(
        functools.partial(local, mesh.shape["row"], mesh.shape["col"]),
        mesh=mesh,
        in_specs=placed,
        out_specs=(P(None, "row", None, None), P(None, "row", None)),
        check_vma=False,
    )
```

time: 35 us -> 32.5 us (0.929); the launches traced: 34.9 us -> 32 us
  Pallas kernels: 33.1 us -> 30.2 us
    pallas_call x1, Pallas kernels: 33.1 us -> 30.2 us  [local(): pl.pallas_call(functools.partial(kernel, n_row, n_col), out_shape=(pltpu....]
where the time goes in v2:
time: 32.5 us; the launch traced here: 32 us
  Pallas kernels  30.2 us (93%)
  local copies, waits for them, and re-layouts  1.12 us (3%)
  between operations  0.64 us (2%)
    pallas_call x1, Pallas kernels, local(): pl.pallas_call(functools.partial(kernel, n_row, n_col), out_shape=(pltpu....  30.2 us
    unnamed x2, local copies, waits for them, and re-layouts  1.12 us

profile of v2, /device:TPU:25, one launch (start us, length us, event | category | flops | bytes accessed | tf_op | source)
XLA Modules:
  0.0 32.0 jit_solution(14387290344454108526)
XLA Ops:
  0.6 30.2 %forward_solve.1 = (f32[1,1,4,1024]{3,2,1,0:T(4,128)S(1)}, f32[1,1,4]{2,1,0:T(1,128)S(1)}) custom-call(f32[1,1,4,1024]{3,2,1,0:T(4,128)} %rhs_hbm.1, bf16[1,1,256,1024]{3,2,1,0:T(8,128)(2,1)} %inv_hbm.1, bf16[1,1,2,1,128,1024]{5,4,3,2,1,0:T(8,128)(2,1)} %u_hbm.1, bf16[1,1,2,1,128,1024]{5,4,3,2,1,0:T(8,128)(2,1)} %v_hbm.1, s32[2]{0:T(128)} %bitcast.1), custom_call_target="tpu_custom_call" | custom-call | tf_op jit(solution)/shard_map/forward_solve/pallas_call | solution.py:773
  30.8 0.6 %copy.9 = f32[1,1,4,1024]{3,2,1,0:T(4,128)} copy(f32[1,1,4,1024]{3,2,1,0:T(4,128)S(1)} %get-tuple-element.2) | data formatting | bytes 32768
  31.4 0.5 %copy.10 = f32[1,1,4]{2,1,0:T(1,128)} copy(f32[1,1,4]{2,1,0:T(1,128)S(1)} %get-tuple-element.3) | data formatting | bytes 32

commit v3 on v2

--- a/solution.py
+++ b/solution.py
@@ -69,7 +69,12 @@
         pltpu.make_async_copy(rhs_hbm.at[0, 0], rhs_ref, in_sem.at[3]),
         pltpu.make_async_copy(rank_hbm, rank_ref, in_sem.at[4]),
     ]
-    for copy in copies:
+    @pl.when(lax.axis_index("row") > 0)
+    def _():
+        copies[0].start()
+        copies[1].start()
+
+    for copy in copies[2:]:
         copy.start()
 
     even = lax.rem(row, 2) == 0
@@ -129,7 +134,7 @@
         return count
 
     def at_once(low, high):
-        return (low == 0) & (high <= NEAR)
+        return (low == 0) & (high == 1)
 
     for peer in peers:
         signal(barrier, row, peer)
@@ -189,8 +194,11 @@
         for s in range(n_col):
             into[s] = tile[:, s * piece:(s + 1) * piece]
 
-    copies[0].wait()
-    copies[1].wait()
+    @pl.when(row > 0)
+    def _():
+        copies[0].wait()
+        copies[1].wait()
+
     copies[4].wait()
 
     @pl.when(hands)
@@ -224,12 +232,16 @@
         across = n_col - 1 - home
         return (across == s) & (across < home) & (cc >= s + half)
 
+    def is_split(home, s):
+        across = n_col - 1 - home
+        return (across == s) & (across < home)
+
     def joined(home, s):
         across = n_col - 1 - home
         return (across > home) & (across == s)
 
     def spread(out, into, recv, target, home, cross):
-        for s in reversed(range(n_col)):
+        for s in range(n_col):
             if s > 0:
 
                 @pl.when(cross & joined(home, s - 1))
@@ -237,7 +249,7 @@
                     remote(out.at[s - 1], out.at[s - 1], v_send.at[s], m_recv.at[s - 1], (row, s)).start()
 
             for cc in range(s, n_col):
-                gone = cross & joined(home, s)
+                gone = cross & (joined(home, s) | is_split(home, s))
                 way = cross & by_way(home, s, cc)
                 later = cross & is_late(home, s, cc)
 
@@ -249,7 +261,21 @@
                 def _():
                     remote(out.at[cc], into.at[cc], v_send.at[s], recv, (target, s)).start()
 
+        for s in range(n_col):
+            for cc in range(s, min(s + half, n_col)):
+
+                @pl.when(cross & is_split(home, s))
+                def _():
+                    remote(out.at[cc], out.at[cc], v_send.at[s], m_recv.at[cc], (row, s)).start()
+
     def spread_late(out, into, recv, target, home):
+        for s in range(1, n_col):
+
+            @pl.when(is_split(home, s - 1))
+            def _():
+                part = pl.ds(s, n_col - s)
+                remote(out.at[part], out.at[part], v_send.at[s], m_recv.at[0], (row, s)).wait_send()
+
         for s in range(n_col):
             for cc in range(min(s + half, n_col), n_col):
 
@@ -261,6 +287,8 @@
         for s in range(n_col):
             part = pl.ds(s, n_col - s)
             gone = cross & joined(home, s)
+            if s > 0:
+                gone = gone | (cross & is_split(home, s - 1))
             more = (cross & joined(home, s - 1)) if s > 0 else jnp.bool_(False)
 
             @pl.when(jnp.logical_not(gone | more))
@@ -279,7 +307,7 @@
         more = joined(home, col - 1)
         first = jnp.where(more, col - 1, col)
         part = jnp.where(across < home, across == col, col < home)
-        stop = jnp.where(joined(home, col), col, jnp.where(part, jnp.minimum(col + half, n_col), n_col))
+        stop = jnp.where(part, jnp.minimum(col + half, n_col), n_col)
 
         def forward(cc, carry):
             remote(out.at[cc], out.at[cc], v_send.at[0], m_recv.at[cc], (row, home)).wait_recv()
@@ -290,7 +318,7 @@
 
             @pl.when(more)
             def _():
-                remote(out.at[cc], into.at[cc], e_send, recv, (target, across)).start()
+                remote(out.at[cc], out.at[cc], e_send, m_recv.at[cc], (row, across)).start()
 
             return carry
 
@@ -300,7 +328,7 @@
         across = n_col - 1 - home
         for cc in range(n_col):
             few = pl.ds(cc, min(half, n_col - cc))
-            here = (col == cc) & jnp.logical_not(joined(home, cc))
+            here = col == cc
             half_way = jnp.where(across < home, across == cc, cc < home)
 
             @pl.when(here & jnp.logical_not(half_way))
@@ -332,17 +360,19 @@
         def _():
             remote(into, into, u_send, recv, (row, home)).wait_recv()
 
-    @pl.when(hands)
+    early_l = (row < FIRST_SHORT) | is_even_end
+
+    @pl.when(hands & early_l)
     def _():
         share(l_out, l_in, k_recv)
 
+    @pl.when(gives)
+    def _():
+        spread(v_out, v_in, v_recv, row - 1, prev_home, crosses)
+
     @pl.when(gives & is_even_end)
     def _():
         share(u_out, u_in, u_recv)
-
-    @pl.when(gives)
-    def _():
-        spread(v_out, v_in, v_recv, row - 1, prev_home, crosses)
 
     @pl.when(gives_far)
     def _():
@@ -390,6 +420,10 @@
 
     pl.when(row > 0)(log_part)
 
+    @pl.when(gives & crosses)
+    def _():
+        spread_late(v_out, v_in, v_recv, row - 1, prev_home)
+
     @pl.when(gives & jnp.logical_not(even))
     def _():
         spread_done(v_out, prev_home, crosses)
@@ -415,10 +449,10 @@
                     preferred_element_type=jnp.float32,
                 )
 
-    def long_step(q, cond):
+    def long_step(q):
         j = q * n_col + col
 
-        @pl.when((j < long_count) & cond)
+        @pl.when(j < long_count)
         def _():
             near = row - j <= near_of(j)
 
@@ -467,8 +501,22 @@
                 remote(p_out.at[q, peer], p_in.at[j], p_send.at[q], p_recv.at[j], (row, peer)).start()
             p_in[j] = p_out[q, col]
 
+    @pl.when(takes | takes_whole)
+    def _():
+        remote(d_in, d_in, d_send, d_recv, (row - 1, col)).wait_recv()
+        d_tile[...] = d_in[...].astype(jnp.bfloat16)
+
+    @pl.when(takes_whole)
+    def _():
+        remote(du_in, du_in, du_send, du_recv, (row - 1, col)).wait_recv()
+        du_tile[...] = du_in[...].astype(jnp.bfloat16)
+
+    @pl.when(is_end & (col != far_home))
+    def _():
+        relay(x_out, x_in, x_recv, row - 2, far_home)
+
     for q in range(per_col):
-        long_step(q, is_even_end & (q * n_col + col <= row - 5))
+        long_step(q)
 
     @pl.when(is_even_end)
     def _():
@@ -482,34 +530,17 @@
             for s in range(n_col):
                 remote(a_out.at[k], a_in.at[k, col], a_send, a_recv, (row + 1, s)).start()
 
-    @pl.when(takes | takes_whole)
-    def _():
-        remote(d_in, d_in, d_send, d_recv, (row - 1, col)).wait_recv()
-        d_tile[...] = d_in[...].astype(jnp.bfloat16)
-
-    @pl.when(takes_whole)
-    def _():
-        remote(du_in, du_in, du_send, du_recv, (row - 1, col)).wait_recv()
-        du_tile[...] = du_in[...].astype(jnp.bfloat16)
-
-    @pl.when(is_end & (col != far_home))
-    def _():
-        relay(x_out, x_in, x_recv, row - 2, far_home)
-
-    for q in range(per_col):
-        long_step(q, jnp.logical_not(is_even_end & (q * n_col + col <= row - 5)))
-
     @pl.when(feeds & jnp.logical_not(is_even_end))
     def _():
         fold_with(v_in, v_recv, fold)
 
-    @pl.when(gives & crosses)
-    def _():
-        spread_late(v_out, v_in, v_recv, row - 1, prev_home)
-
     @pl.when(gives & crosses & jnp.logical_not(is_even_end))
     def _():
         share(u_out, u_in, u_recv)
+
+    @pl.when(hands & jnp.logical_not(early_l))
+    def _():
+        share(l_out, l_in, k_recv)
 
     @pl.when(gives_far)
     def _():
@@ -630,10 +661,16 @@
 
         return carry
 
-    lax.fori_loop(row + 1, near_end, send_y, 0)
+    first = row == 0
+    lax.fori_loop(row + 1, jnp.where(first, 2, near_end), send_y, 0)
     for peer in peers:
         remote(y_row.at[col], y_row.at[col], o_send, o_recv, (row, peer)).start()
-    pl.when(row == 0)(log_part)
+
+    @pl.when(first)
+    def _():
+        log_part()
+        pl.semaphore_wait(ready, answers)
+        lax.fori_loop(2, near_end, send_y, 0)
 
     remote(logs.at[others], logs.at[others], l_send, l_recv, (row, peers[0])).wait()
     log_sum = logs[0]
@@ -725,10 +762,6 @@
     def send_far(i, carry):
         far_copy(i).start()
         return carry
-
-    @pl.when((row == 0) & (answers > 0))
-    def _():
-        pl.semaphore_wait(ready, answers)
 
     lax.fori_loop(jnp.where(relays, near_end, n_row), n_row, send_far, 0)
     white_ref[0, 0] = y

time: 32.5 us -> 31.5 us (0.969)
  Pallas kernels: 30.2 us -> 29.2 us
    pallas_call x1, Pallas kernels: 30.2 us -> 29.2 us  [local(): pl.pallas_call(functools.partial(kernel, n_row, n_col), out_shape=(pltpu....]
where the time goes in v3:
time: 31.5 us; the launch traced here: 31 us
  Pallas kernels  29.2 us (93%)
  local copies, waits for them, and re-layouts  1.12 us (4%)
  between operations  0.64 us (2%)
    pallas_call x1, Pallas kernels, local(): pl.pallas_call(functools.partial(kernel, n_row, n_col), out_shape=(pltpu....  29.2 us
    unnamed x2, local copies, waits for them, and re-layouts  1.12 us

profile of v3, /device:TPU:25, one launch (start us, length us, event | category | flops | bytes accessed | tf_op | source)
XLA Modules:
  0.0 31.0 jit_solution(4812015165121836994)
XLA Ops:
  0.6 29.2 %forward_solve.1 = (f32[1,1,4,1024]{3,2,1,0:T(4,128)S(1)}, f32[1,1,4]{2,1,0:T(1,128)S(1)}) custom-call(f32[1,1,4,1024]{3,2,1,0:T(4,128)} %rhs_hbm.1, bf16[1,1,256,1024]{3,2,1,0:T(8,128)(2,1)} %inv_hbm.1, bf16[1,1,2,1,128,1024]{5,4,3,2,1,0:T(8,128)(2,1)} %u_hbm.1, bf16[1,1,2,1,128,1024]{5,4,3,2,1,0:T(8,128)(2,1)} %v_hbm.1, s32[2]{0:T(128)} %bitcast.1), custom_call_target="tpu_custom_call" | custom-call | tf_op jit(solution)/shard_map/forward_solve/pallas_call | solution.py:806
  29.8 0.6 %copy.9 = f32[1,1,4,1024]{3,2,1,0:T(4,128)} copy(f32[1,1,4,1024]{3,2,1,0:T(4,128)S(1)} %get-tuple-element.2) | data formatting | bytes 32768
  30.5 0.5 %copy.10 = f32[1,1,4]{2,1,0:T(1,128)} copy(f32[1,1,4]{2,1,0:T(1,128)S(1)} %get-tuple-element.3) | data formatting | bytes 32

commit v4 on v3

--- a/solution.py
+++ b/solution.py
@@ -46,6 +46,7 @@
     nrhs = rhs_ref.shape[0]
     piece = width // n_col
     half = n_col // 2
+    some = max(n_col // 4, 1)
     peers = [lax.rem(col + k, n_col) for k in range(1, n_col)]
     others = pl.ds(0, n_col - 1)
     own_slot = row // n_col
@@ -65,7 +66,7 @@
     copies = [
         pltpu.make_async_copy(v_hbm.at[0, 0, :, 0], v_ref, in_sem.at[0]),
         pltpu.make_async_copy(u_hbm.at[0, 0, :, 0], u_ref, in_sem.at[1]),
-        pltpu.make_async_copy(inv_hbm.at[0, 0], inv_ref, in_sem.at[2]),
+        None,
         pltpu.make_async_copy(rhs_hbm.at[0, 0], rhs_ref, in_sem.at[3]),
         pltpu.make_async_copy(rank_hbm, rank_ref, in_sem.at[4]),
     ]
@@ -74,8 +75,27 @@
         copies[0].start()
         copies[1].start()
 
-    for copy in copies[2:]:
+    def tail_of(c):
+        start = c * piece // 128 * 128
+        return pl.ds(start, width - start)
+
+    def inverse_copy(c):
+        return pltpu.make_async_copy(inv_hbm.at[0, 0, :, tail_of(c)], inv_ref.at[:, tail_of(c)], in_sem.at[2])
+
+    def by_col(act):
+        for c in range(n_col):
+            pl.when(col == c)(functools.partial(act, c))
+
+    by_col(lambda c: inverse_copy(c).start())
+    for copy in copies[3:]:
         copy.start()
+
+    for s in range(1, n_col):
+        start = s * piece // 128 * 128
+        if start:
+            y_row[s, :, :start] = jnp.zeros((nrhs, start), jnp.float32)
+            for q in range(per_col):
+                y_in[q, s, :, :start] = jnp.zeros((nrhs, start), jnp.float32)
 
     even = lax.rem(row, 2) == 0
     short = row >= FIRST_SHORT
@@ -226,11 +246,14 @@
 
     def by_way(home, s, cc):
         across = n_col - 1 - home
-        return (home != s) & jnp.where(across < home, (across != s) | (cc < s + half), (s > home) | (cc < s + half))
+        return (home != s) & jnp.where(across < home, (across != s) | (cc < s + some), (s > home) | (cc < s + half))
 
     def is_late(home, s, cc):
         across = n_col - 1 - home
-        return (across == s) & (across < home) & (cc >= s + half)
+        return (across == s) & (across < home) & (cc >= s + some)
+
+    def split_row(home):
+        return n_col - 1 - home < home
 
     def is_split(home, s):
         across = n_col - 1 - home
@@ -262,22 +285,22 @@
                     remote(out.at[cc], into.at[cc], v_send.at[s], recv, (target, s)).start()
 
         for s in range(n_col):
-            for cc in range(s, min(s + half, n_col)):
+            for cc in range(s, min(s + some, n_col)):
 
                 @pl.when(cross & is_split(home, s))
                 def _():
                     remote(out.at[cc], out.at[cc], v_send.at[s], m_recv.at[cc], (row, s)).start()
 
     def spread_late(out, into, recv, target, home):
-        for s in range(1, n_col):
-
-            @pl.when(is_split(home, s - 1))
+        for s in range(n_col - 1):
+
+            @pl.when(split_row(home) & (home == s + 1))
             def _():
                 part = pl.ds(s, n_col - s)
                 remote(out.at[part], out.at[part], v_send.at[s], m_recv.at[0], (row, s)).wait_send()
 
         for s in range(n_col):
-            for cc in range(min(s + half, n_col), n_col):
+            for cc in range(min(s + some, n_col), n_col):
 
                 @pl.when(is_late(home, s, cc))
                 def _():
@@ -287,8 +310,7 @@
         for s in range(n_col):
             part = pl.ds(s, n_col - s)
             gone = cross & joined(home, s)
-            if s > 0:
-                gone = gone | (cross & is_split(home, s - 1))
+            gone = gone | (cross & split_row(home) & (home == s + 1))
             more = (cross & joined(home, s - 1)) if s > 0 else jnp.bool_(False)
 
             @pl.when(jnp.logical_not(gone | more))
@@ -307,7 +329,8 @@
         more = joined(home, col - 1)
         first = jnp.where(more, col - 1, col)
         part = jnp.where(across < home, across == col, col < home)
-        stop = jnp.where(part, jnp.minimum(col + half, n_col), n_col)
+        share_of = jnp.where(across < home, some, half)
+        stop = jnp.where(part, jnp.minimum(col + share_of, n_col), n_col)
 
         def forward(cc, carry):
             remote(out.at[cc], out.at[cc], v_send.at[0], m_recv.at[cc], (row, home)).wait_recv()
@@ -327,7 +350,6 @@
     def relay_done(out, home):
         across = n_col - 1 - home
         for cc in range(n_col):
-            few = pl.ds(cc, min(half, n_col - cc))
             here = col == cc
             half_way = jnp.where(across < home, across == cc, cc < home)
 
@@ -336,9 +358,12 @@
                 part = pl.ds(cc, n_col - cc)
                 remote(out.at[part], out.at[part], f_send, v_recv, (row, home)).wait_send()
 
-            @pl.when(here & half_way)
-            def _():
-                remote(out.at[few], out.at[few], f_send, v_recv, (row, home)).wait_send()
+            for count, cond in ((some, across < home), (half, across > home)):
+                few = pl.ds(cc, min(count, n_col - cc))
+
+                @pl.when(here & half_way & cond)
+                def _():
+                    remote(out.at[few], out.at[few], f_send, v_recv, (row, home)).wait_send()
 
             if cc > 0:
 
@@ -394,7 +419,7 @@
     def _():
         relay(v_out, v_in, v_recv, row - 1, prev_home)
 
-    copies[2].wait()
+    by_col(lambda c: inverse_copy(c).wait())
     copies[3].wait()
 
     for cc in range(n_col):
@@ -458,7 +483,9 @@
 
             @pl.when(near)
             def _():
-                remote(y_in.at[q], y_in.at[q], y_send.at[0], y_recv.at[q], (j, col)).wait_recv()
+                for s in range(n_col):
+                    part = y_in.at[q, s, :, tail_of(s)]
+                    remote(part, part, y_send.at[0], y_recv.at[q, s], (j, col)).wait_recv()
                 y = y_in[q, 0]
                 for s in range(1, n_col):
                     y = y + y_in[q, s]
@@ -466,7 +493,7 @@
 
             @pl.when(jnp.logical_not(near))
             def _():
-                remote(y_in.at[q, 0], y_in.at[q, 0], y_send.at[0], y_recv.at[q], (j, col)).wait_recv()
+                remote(y_in.at[q, 0], y_in.at[q, 0], y_send.at[0], y_recv.at[q, 0], (j, col)).wait_recv()
                 y_full[...] = y_in[q, 0]
 
             y = y_full[...].astype(jnp.bfloat16)
@@ -649,22 +676,33 @@
 
         send_w(w_out, w_in, w_send, w_recv, row + 1)
 
-    y_row[col] = jnp.dot(reduced, inv_ref[...], preferred_element_type=jnp.float32)
-
-    def near_copy(i):
-        return remote(y_row.at[col], y_in.at[own_slot, col], y_send.at[i], y_recv.at[own_slot], (i, own_home))
+    def own_part(c):
+        tail = tail_of(c)
+        y_row[c, :, tail] = jnp.dot(reduced, inv_ref[:, tail], preferred_element_type=jnp.float32)
+
+    by_col(own_part)
+
+    def near_copy(i, c):
+        tail = tail_of(c)
+        return remote(
+            y_row.at[c, :, tail], y_in.at[own_slot, c, :, tail], y_send.at[i], y_recv.at[own_slot, c], (i, own_home)
+        )
 
     def send_y(i, carry):
         @pl.when(row < longs_of(i))
         def _():
-            near_copy(i).start()
+            by_col(lambda c: near_copy(i, c).start())
 
         return carry
+
+    def own_copy(c, peer):
+        part = y_row.at[c, :, tail_of(c)]
+        return remote(part, part, o_send, o_recv.at[c], (row, peer))
 
     first = row == 0
     lax.fori_loop(row + 1, jnp.where(first, 2, near_end), send_y, 0)
     for peer in peers:
-        remote(y_row.at[col], y_row.at[col], o_send, o_recv, (row, peer)).start()
+        by_col(lambda c: own_copy(c, peer).start())
 
     @pl.when(first)
     def _():
@@ -681,7 +719,7 @@
     def left_y(i, carry):
         @pl.when(row < longs_of(i))
         def _():
-            near_copy(i).wait_send()
+            by_col(lambda c: near_copy(i, c).wait_send())
 
         return carry
 
@@ -750,14 +788,19 @@
             part = p_out.at[q, others]
             remote(part, part, p_send.at[q], p_recv.at[0], (row, peers[0])).wait_send()
 
-    remote(y_row.at[others], y_row.at[others], o_send, o_recv, (row, peers[0])).wait_recv()
+    for s in range(n_col):
+
+        @pl.when(col != s)
+        def _():
+            own_copy(s, peers[0]).wait_recv()
+
     y = y_row[0]
     for s in range(1, n_col):
         y = y + y_row[s]
     y_all[...] = y
 
     def far_copy(i):
-        return remote(y_all, y_in.at[own_slot, 0], y_send.at[i], y_recv.at[own_slot], (i, col))
+        return remote(y_all, y_in.at[own_slot, 0], y_send.at[i], y_recv.at[own_slot, 0], (i, col))
 
     def send_far(i, carry):
         far_copy(i).start()
@@ -777,7 +820,12 @@
         return carry
 
     lax.fori_loop(jnp.where(relays, near_end, n_row), n_row, left_far, 0)
-    remote(y_row.at[others], y_row.at[others], o_send, o_recv, (row, peers[0])).wait_send()
+
+    def own_left(c):
+        part = y_row.at[others, :, tail_of(c)]
+        remote(part, part, o_send, o_recv.at[c], (row, peers[0])).wait_send()
+
+    by_col(own_left)
 
 
 def local(n_row, n_col, right_side, inverse_t, u_factor, v_factor, ranks):
@@ -844,10 +892,10 @@
             bf16(2, rank_max, rank_max),
             dma((5,)),
             dma((n_row,)),
-            dma((per_col,)),
+            dma((per_col, n_col)),
             dma((per_col,)),
             dma((n_row,)),
-            dma, dma, dma, dma,
+            dma, dma((n_col,)), dma, dma,
             dma((n_col,)),
             dma, dma, dma, dma, dma,
             dma((n_col,)),

time: 31.5 us -> 30.5 us (0.968)
  Pallas kernels: 29.2 us -> 28.4 us
    pallas_call x1, Pallas kernels: 29.2 us -> 28.4 us  [local(): pl.pallas_call(functools.partial(kernel, n_row, n_col), out_shape=(pltpu....]
where the time goes in v4:
time: 30.5 us; the launch traced here: 30.1 us
  Pallas kernels  28.4 us (93%)
  local copies, waits for them, and re-layouts  1.12 us (4%)
  between operations  0.64 us (2%)
    pallas_call x1, Pallas kernels, local(): pl.pallas_call(functools.partial(kernel, n_row, n_col), out_shape=(pltpu....  28.4 us
    unnamed x2, local copies, waits for them, and re-layouts  1.12 us

profile of v4, /device:TPU:25, one launch (start us, length us, event | category | flops | bytes accessed | tf_op | source)
XLA Modules:
  0.0 30.1 jit_solution(12093564529658545015)
XLA Ops:
  0.6 28.4 %forward_solve.1 = (f32[1,1,4,1024]{3,2,1,0:T(4,128)S(1)}, f32[1,1,4]{2,1,0:T(1,128)S(1)}) custom-call(f32[1,1,4,1024]{3,2,1,0:T(4,128)} %rhs_hbm.1, bf16[1,1,256,1024]{3,2,1,0:T(8,128)(2,1)} %inv_hbm.1, bf16[1,1,2,1,128,1024]{5,4,3,2,1,0:T(8,128)(2,1)} %u_hbm.1, bf16[1,1,2,1,128,1024]{5,4,3,2,1,0:T(8,128)(2,1)} %v_hbm.1, s32[2]{0:T(128)} %bitcast.1), custom_call_target="tpu_custom_call" | custom-call | tf_op jit(solution)/shard_map/forward_solve/pallas_call | solution.py:854
  29.0 0.6 %copy.9 = f32[1,1,4,1024]{3,2,1,0:T(4,128)} copy(f32[1,1,4,1024]{3,2,1,0:T(4,128)S(1)} %get-tuple-element.2) | data formatting | bytes 32768
  29.6 0.5 %copy.10 = f32[1,1,4]{2,1,0:T(1,128)} copy(f32[1,1,4]{2,1,0:T(1,128)S(1)} %get-tuple-element.3) | data formatting | bytes 32

commit v5 on v4

--- a/solution.py
+++ b/solution.py
@@ -35,6 +35,7 @@
     x_out, x_in, t_out, t_in, fold_x, wx_out, wx_in,
     d_out, d_in, d_tile, du_out, du_in, du_tile, pd_out, l_out, l_in, wl_out, wl_in, we_in,
     a_out, a_in, a_sum,
+    hl_in, hu_in, hf_in, hv_out, hv_in, hv_tile, hb_out, hb_in, hz_out, hz_in, hw_out, hw_in, hy_out,
     in_sem, y_send, y_recv, p_send, p_recv, o_send, o_recv, l_send, l_recv,
     v_send, v_recv, u_send, u_recv, w_send, w_recv, m_recv, f_send, e_send, ready,
     x_recv, t_recv, k_recv, d_send, d_recv, du_send, du_recv, pd_send, wl_send, wl_recv, wp_send,
@@ -103,6 +104,8 @@
     is_end = row == end
     is_even_end = row == even_end
     is_ahead = row == ahead
+    lent = row == ahead - 1
+    before = row == ahead - 2
     long_count = longs_of(row)
     near_end = jnp.minimum(row + near_of(row) + 1, n_row)
     relays = col == own_home
@@ -123,7 +126,7 @@
     def above(act):
         yield row + 1, row_of(row + 1, row < end, act)
         for d in range(2, NEAR + 2):
-            wide = is_ahead if d == 2 else jnp.bool_(False)
+            wide = (is_ahead | before) if d == 2 else jnp.bool_(False)
             one = (row + d < n_row) & (d <= near_of(row)) & jnp.logical_not(wide)
 
             @pl.when(one)
@@ -140,7 +143,7 @@
         for d in range(2, NEAR + 2):
             fed = (row >= d) & (d <= near_of(row - d)) & (lax.rem(jnp.maximum(row - d, 0), n_col) == col)
             if d == 2:
-                fed = fed | is_end
+                fed = fed | is_end | is_ahead
             count += row_of(row - d, fed, act)
         for q in range(per_col):
             j = q * n_col + col
@@ -395,7 +398,7 @@
     def _():
         spread(v_out, v_in, v_recv, row - 1, prev_home, crosses)
 
-    @pl.when(gives & is_even_end)
+    @pl.when(gives & (is_even_end | jnp.logical_not(even)))
     def _():
         share(u_out, u_in, u_recv)
 
@@ -421,6 +424,18 @@
 
     by_col(lambda c: inverse_copy(c).wait())
     copies[3].wait()
+
+    def lend(src, dst, send, recv):
+        return remote(src, dst, send, recv, (row + 1, col))
+
+    def lend_inverse(c):
+        return lend(hv_out.at[:, tail_of(c)], hv_in.at[:, tail_of(c)], wl_send, wx_recv)
+
+    def lend_tail(c):
+        hv_out[:, tail_of(c)] = inv_ref[:, tail_of(c)].astype(jnp.float32)
+        lend_inverse(c).start()
+
+    pl.when(lent)(functools.partial(by_col, lend_tail))
 
     for cc in range(n_col):
 
@@ -449,11 +464,6 @@
     def _():
         spread_late(v_out, v_in, v_recv, row - 1, prev_home)
 
-    @pl.when(gives & jnp.logical_not(even))
-    def _():
-        spread_done(v_out, prev_home, crosses)
-        share(u_out, u_in, u_recv)
-
     def fold_with(into, recv, target):
         target[...] = jnp.zeros_like(target)
         for cc in range(n_col):
@@ -474,10 +484,10 @@
                     preferred_element_type=jnp.float32,
                 )
 
-    def long_step(q):
+    def long_step(q, cond):
         j = q * n_col + col
 
-        @pl.when(j < long_count)
+        @pl.when((j < long_count) & cond)
         def _():
             near = row - j <= near_of(j)
 
@@ -501,10 +511,12 @@
             @pl.when(takes & (j == theirs))
             def _():
                 wl_out[...] = lax.dot_general(y, d_tile[...], NT, preferred_element_type=jnp.float32)
-                for s in range(n_col):
-                    remote(wl_out, wl_in, wl_send, wl_recv, (row - 1, s)).start()
-
-                @pl.when(is_end)
+                @pl.when(jnp.logical_not(is_ahead))
+                def _():
+                    for s in range(n_col):
+                        remote(wl_out, wl_in, wl_send, wl_recv, (row - 1, s)).start()
+
+                @pl.when(is_end | is_ahead)
                 def _():
                     for peer in peers:
                         remote(wl_out, wl_in, wp_send, wl_recv, (row, peer)).start()
@@ -543,7 +555,66 @@
         relay(x_out, x_in, x_recv, row - 2, far_home)
 
     for q in range(per_col):
-        long_step(q)
+        long_step(q, jnp.logical_not(is_ahead & (q * n_col + col == row - 2)))
+
+    def send_w(out, into, send, recv, i):
+        for s in range(n_col):
+            remote(out, into.at[col], send, recv, (i, s)).start()
+
+    def wait_w(into, send, recv, i):
+        remote(into, into, send, recv, (i, 0)).wait_recv()
+        total = into[0]
+        for s in range(1, n_col):
+            total = total + into[s]
+        return total
+
+    def borrowed_y(c):
+        tail = tail_of(c)
+        slot = (ahead - 1) // n_col
+        home = (ahead - 1) % n_col
+        return remote(hy_out.at[:, tail], y_in.at[slot, c, :, tail], y_send.at[end], y_recv.at[slot, c], (end, home))
+
+    @pl.when(is_ahead)
+    def _():
+        back = (row - 1, col)
+        by_col(lambda c: remote(hv_in.at[:, tail_of(c)], hv_in.at[:, tail_of(c)], wl_send, wx_recv, back).wait_recv())
+        by_col(lambda c: hv_tile.__setitem__((slice(None), tail_of(c)), hv_in[:, tail_of(c)].astype(jnp.bfloat16)))
+        remote(hl_in, hl_in, a_send, k_recv, back).wait_recv()
+        remote(hu_in, hu_in, we_send, a_recv, back).wait_recv()
+        remote(hf_in, hf_in, wx_send, we_recv, back).wait_recv()
+        remote(hb_in, hb_in, wp_send, t_recv, back).wait_recv()
+        l_part = hl_in[...].astype(jnp.bfloat16)
+        u_part = hu_in[...].astype(jnp.bfloat16)
+        factor = hf_in[...].astype(jnp.bfloat16)
+
+        @pl.when(answers > 0)
+        def _():
+            pl.semaphore_wait(ready, answers)
+
+        @pl.when(jnp.logical_not(takes))
+        def _():
+            remote(wl_in, wl_in, wp_send, wl_recv, (row, their_home)).wait_recv()
+
+        part = hb_in[...] - jnp.dot(wl_in[...].astype(jnp.bfloat16), l_part, preferred_element_type=jnp.float32)
+        inner = wait_w(hw_in, w_send, du_recv, row - 2)
+        part -= jnp.dot(inner.astype(jnp.bfloat16), u_part, preferred_element_type=jnp.float32)
+        part = part.astype(jnp.bfloat16)
+        hw_out[...] = jnp.dot(part, factor, preferred_element_type=jnp.float32)
+        for peer in peers:
+            remote(hw_out, w_in.at[col], a_send, w_recv, (row, peer)).start()
+        w_in[col] = hw_out[...]
+
+        def borrowed_part(c):
+            tail = tail_of(c)
+            hy_out[:, tail] = jnp.dot(part, hv_tile[:, tail], preferred_element_type=jnp.float32)
+            borrowed_y(c).start()
+
+        by_col(borrowed_part)
+        hz_out[...] = part.astype(jnp.float32)
+        remote(hz_out, hz_in, pd_send, du_recv, back).start()
+
+    for q in range(per_col):
+        long_step(q, is_ahead & (q * n_col + col == row - 2))
 
     @pl.when(is_even_end)
     def _():
@@ -561,6 +632,10 @@
     def _():
         fold_with(v_in, v_recv, fold)
 
+        @pl.when(lent)
+        def _():
+            lend(fold, hf_in, wx_send, we_recv).start()
+
     @pl.when(gives & crosses & jnp.logical_not(is_even_end))
     def _():
         share(u_out, u_in, u_recv)
@@ -598,28 +673,28 @@
 
     base[...] = lax.fori_loop(0, long_count, gather_p, base[...])
 
+    @pl.when(lent)
+    def _():
+        hb_out[...] = base[...]
+        lend(hb_out, hb_in, wp_send, t_recv).start()
+        shared_wait(l_in, k_recv, mine_home)
+        lend(l_in, hl_in, a_send, k_recv).start()
+        shared_wait(u_in, u_recv, prev_home)
+        lend(u_in, hu_in, we_send, a_recv).start()
+        remote(hz_in, hz_in, pd_send, du_recv, (row + 1, col)).wait_recv()
+        base[...] = hz_in[...]
+
     @pl.when(is_even_end)
     def _():
         remote(p_in.at[whole], p_in.at[whole], p_send.at[0], p_recv.at[whole], (row + 1, whole_home)).wait_recv()
         base[...] -= p_in[whole]
 
-    def send_w(out, into, send, recv, i):
-        for s in range(n_col):
-            remote(out, into.at[col], send, recv, (i, s)).start()
-
-    def wait_w(into, send, recv, i):
-        remote(into, into, send, recv, (i, 0)).wait_recv()
-        total = into[0]
-        for s in range(1, n_col):
-            total = total + into[s]
-        return total
-
     @pl.when(is_even_end)
     def _():
         w_out[...] = jnp.dot(base[...].astype(jnp.bfloat16), fold[...].astype(jnp.bfloat16), preferred_element_type=jnp.float32)
         send_w(w_out, w_in, w_send, w_recv, row + 1)
 
-    @pl.when(handed)
+    @pl.when(handed & jnp.logical_not(lent))
     def _():
         @pl.when(jnp.logical_not(is_even_end))
         def _():
@@ -629,7 +704,18 @@
         remote(wl_in, wl_in, wl_send, wl_recv, (row + 1, mine_home)).wait_recv()
         base[...] -= jnp.dot(wl_in[...].astype(jnp.bfloat16), l_part, preferred_element_type=jnp.float32)
 
-    @pl.when(short & jnp.logical_not(is_end))
+    @pl.when(is_ahead)
+    def _():
+        shared_wait(u_in, u_recv, prev_home)
+        u_part = u_in[...].astype(jnp.bfloat16)
+        part = w_in.at[others]
+        remote(part, part, a_send, w_recv, (row, peers[0])).wait_recv()
+        inner = w_in[0]
+        for s in range(1, n_col):
+            inner = inner + w_in[s]
+        base[...] -= jnp.dot(inner.astype(jnp.bfloat16), u_part, preferred_element_type=jnp.float32)
+
+    @pl.when(short & jnp.logical_not(is_end | is_ahead | lent))
     def _():
         @pl.when(jnp.logical_not(is_even_end))
         def _():
@@ -660,11 +746,11 @@
 
     reduced = base[...].astype(jnp.bfloat16)
 
-    @pl.when((jnp.logical_not(even)) & (answers > 0))
+    @pl.when(jnp.logical_not(even | is_ahead) & (answers > 0))
     def _():
         pl.semaphore_wait(ready, answers)
 
-    @pl.when(feeds & jnp.logical_not(is_even_end))
+    @pl.when(feeds & jnp.logical_not(is_even_end | lent))
     def _():
         w_out[...] = jnp.dot(reduced, fold[...].astype(jnp.bfloat16), preferred_element_type=jnp.float32)
 
@@ -674,7 +760,13 @@
             wx_out[...] = jnp.dot(reduced, fold_x[...].astype(jnp.bfloat16), preferred_element_type=jnp.float32)
             send_w(wx_out, wx_in, wx_send, wx_recv, row + 2)
 
-        send_w(w_out, w_in, w_send, w_recv, row + 1)
+        @pl.when(before)
+        def _():
+            send_w(w_out, hw_in, w_send, du_recv, row + 2)
+
+        @pl.when(jnp.logical_not(before))
+        def _():
+            send_w(w_out, w_in, w_send, w_recv, row + 1)
 
     def own_part(c):
         tail = tail_of(c)
@@ -689,7 +781,7 @@
         )
 
     def send_y(i, carry):
-        @pl.when(row < longs_of(i))
+        @pl.when((row < longs_of(i)) & jnp.logical_not(lent))
         def _():
             by_col(lambda c: near_copy(i, c).start())
 
@@ -717,7 +809,7 @@
     log_term = log_sum * (1.0 / width) - 0.5 * math.log(2.0 * math.pi)
 
     def left_y(i, carry):
-        @pl.when(row < longs_of(i))
+        @pl.when((row < longs_of(i)) & jnp.logical_not(lent))
         def _():
             by_col(lambda c: near_copy(i, c).wait_send())
 
@@ -725,12 +817,24 @@
 
     lax.fori_loop(row + 1, near_end, left_y, 0)
 
-    @pl.when(feeds)
+    @pl.when(feeds & jnp.logical_not(lent))
     def _():
         remote(w_in, w_in, w_send, w_recv, (row + 1, 0)).wait_send()
 
+    @pl.when(lent)
+    def _():
+        by_col(lambda c: lend_inverse(c).wait_send())
+        lend(fold, hf_in, wx_send, we_recv).wait_send()
+        lend(hb_out, hb_in, wp_send, t_recv).wait_send()
+        lend(l_in, hl_in, a_send, k_recv).wait_send()
+        lend(u_in, hu_in, we_send, a_recv).wait_send()
+
     @pl.when(is_ahead)
     def _():
+        part = w_in.at[others]
+        remote(part, part, a_send, w_recv, (row, peers[0])).wait_send()
+        by_col(lambda c: borrowed_y(c).wait_send())
+        remote(hz_out, hz_in, pd_send, du_recv, (row - 1, col)).wait_send()
         remote(w_in, w_in, we_send, we_recv, (row + 2, 0)).wait_send()
         remote(w_in, w_in, wx_send, wx_recv, (row + 2, 0)).wait_send()
 
@@ -740,9 +844,11 @@
 
     @pl.when(takes)
     def _():
-        remote(w_in, w_in, wl_send, wl_recv, (row - 1, 0)).wait_send()
-
-        @pl.when(is_end)
+        @pl.when(jnp.logical_not(is_ahead))
+        def _():
+            remote(w_in, w_in, wl_send, wl_recv, (row - 1, 0)).wait_send()
+
+        @pl.when(is_end | is_ahead)
         def _():
             remote(w_in.at[others], w_in.at[others], wp_send, wl_recv, (row, peers[0])).wait_send()
 
@@ -760,12 +866,9 @@
     def _():
         remote(pd_out, pd_out, pd_send, p_recv.at[0], (row - 1, 0)).wait_send()
 
-    @pl.when(gives & even)
+    @pl.when(gives)
     def _():
         spread_done(v_out, prev_home, crosses)
-
-    @pl.when(gives)
-    def _():
         share_done(u_out)
 
     @pl.when(gives_far)
@@ -890,6 +993,19 @@
             f32(2, rank_max, rank_max),
             f32(2, n_col, rank_max, rank_max),
             bf16(2, rank_max, rank_max),
+            f32(rank_max, piece),
+            f32(rank_max, piece),
+            f32(piece, rank_max),
+            f32(piece, width),
+            f32(piece, width),
+            bf16(piece, width),
+            f32(nrhs, piece),
+            f32(nrhs, piece),
+            f32(nrhs, piece),
+            f32(nrhs, piece),
+            f32(nrhs, rank_max),
+            f32(n_col, nrhs, rank_max),
+            f32(nrhs, width),
             dma((5,)),
             dma((n_row,)),
             dma((per_col, n_col)),

time: 30.5 us -> 30.2 us (level)
  no operation moved by 1% of the time
where the time goes in v5:
time: 30.2 us; the launch traced here: 30.1 us
  Pallas kernels  28.3 us (94%)
  local copies, waits for them, and re-layouts  1.12 us (4%)
  between operations  0.64 us (2%)
    pallas_call x1, Pallas kernels, local(): pl.pallas_call(functools.partial(kernel, n_row, n_col), out_shape=(pltpu....  28.3 us
    unnamed x2, local copies, waits for them, and re-layouts  1.12 us

profile of v5, /device:TPU:25, one launch (start us, length us, event | category | flops | bytes accessed | tf_op | source)
XLA Modules:
  0.0 30.1 jit_solution(10849081711683557355)
XLA Ops:
  0.6 28.3 %forward_solve.1 = (f32[1,1,4,1024]{3,2,1,0:T(4,128)S(1)}, f32[1,1,4]{2,1,0:T(1,128)S(1)}) custom-call(f32[1,1,4,1024]{3,2,1,0:T(4,128)} %rhs_hbm.1, bf16[1,1,256,1024]{3,2,1,0:T(8,128)(2,1)} %inv_hbm.1, bf16[1,1,2,1,128,1024]{5,4,3,2,1,0:T(8,128)(2,1)} %u_hbm.1, bf16[1,1,2,1,128,1024]{5,4,3,2,1,0:T(8,128)(2,1)} %v_hbm.1, s32[2]{0:T(128)} %bitcast.1), custom_call_target="tpu_custom_call" | custom-call | tf_op jit(solution)/shard_map/forward_solve/pallas_call | solution.py:957
  28.9 0.6 %copy.9 = f32[1,1,4,1024]{3,2,1,0:T(4,128)} copy(f32[1,1,4,1024]{3,2,1,0:T(4,128)S(1)} %get-tuple-element.2) | data formatting | bytes 32768
  29.5 0.5 %copy.10 = f32[1,1,4]{2,1,0:T(1,128)} copy(f32[1,1,4]{2,1,0:T(1,128)S(1)} %get-tuple-element.3) | data formatting | bytes 32

commit v6 on v5

--- a/solution.py
+++ b/solution.py
@@ -33,7 +33,7 @@
     y_in, p_out, p_in, y_row, logs, base, y_full, y_all,
     v_out, v_in, u_out, u_in, fold, w_out, w_in,
     x_out, x_in, t_out, t_in, fold_x, wx_out, wx_in,
-    d_out, d_in, d_tile, du_out, du_in, du_tile, pd_out, l_out, l_in, wl_out, wl_in, we_in,
+    d_out, d_in, d_tile, vt_ref, l2_in, w2_out, w2_in, l_out, l_in, wl_out, wl_in, we_in,
     a_out, a_in, a_sum,
     hl_in, hu_in, hf_in, hv_out, hv_in, hv_tile, hb_out, hb_in, hz_out, hz_in, hw_out, hw_in, hy_out,
     in_sem, y_send, y_recv, p_send, p_recv, o_send, o_recv, l_send, l_recv,
@@ -47,6 +47,7 @@
     nrhs = rhs_ref.shape[0]
     piece = width // n_col
     half = n_col // 2
+    y_sends = y_send.shape[0]
     some = max(n_col // 4, 1)
     peers = [lax.rem(col + k, n_col) for k in range(1, n_col)]
     others = pl.ds(0, n_col - 1)
@@ -232,7 +233,7 @@
     @pl.when(hands_whole)
     def _():
         d_out[...] = v_ref[whole_slot].astype(jnp.float32)
-        du_out[...] = masked_u(whole_slot)
+        cut(masked_u(whole_slot), l_out)
 
     @pl.when(gives)
     def _():
@@ -394,6 +395,10 @@
     def _():
         share(l_out, l_in, k_recv)
 
+    @pl.when(hands_whole)
+    def _():
+        share(l_out, l2_in, du_recv)
+
     @pl.when(gives)
     def _():
         spread(v_out, v_in, v_recv, row - 1, prev_home, crosses)
@@ -414,11 +419,9 @@
     def _():
         remote(d_out, d_in, d_send, d_recv, (row + 1, col)).start()
 
-    @pl.when(hands_whole)
-    def _():
-        remote(du_out, du_in, du_send, du_recv, (row + 1, col)).start()
-
-    @pl.when(crosses & (col != prev_home))
+    relays_late = is_even_end & joined(prev_home, col)
+
+    @pl.when(crosses & (col != prev_home) & jnp.logical_not(relays_late))
     def _():
         relay(v_out, v_in, v_recv, row - 1, prev_home)
 
@@ -459,6 +462,12 @@
             remote(logs.at[col], logs.at[col], l_send, l_recv, (row, peer)).start()
 
     pl.when(row > 0)(log_part)
+
+    for q in range(per_col):
+
+        @pl.when(q * n_col + col < long_count)
+        def _():
+            vt_ref[q] = v_ref[q].astype(jnp.float32).T.astype(jnp.bfloat16)
 
     @pl.when(gives & crosses)
     def _():
@@ -510,7 +519,7 @@
 
             @pl.when(takes & (j == theirs))
             def _():
-                wl_out[...] = lax.dot_general(y, d_tile[...], NT, preferred_element_type=jnp.float32)
+                wl_out[...] = jnp.dot(y, d_tile[...], preferred_element_type=jnp.float32)
                 @pl.when(jnp.logical_not(is_ahead))
                 def _():
                     for s in range(n_col):
@@ -524,13 +533,14 @@
 
             @pl.when(takes_whole & (j == whole))
             def _():
-                inner = lax.dot_general(y, d_tile[...], NT, preferred_element_type=jnp.float32)
-                p = jnp.dot(inner.astype(jnp.bfloat16), du_tile[...], preferred_element_type=jnp.float32)
+                w2_out[...] = jnp.dot(y, d_tile[...], preferred_element_type=jnp.float32)
                 for s in range(n_col):
-                    pd_out[s] = p[:, s * piece:(s + 1) * piece]
-                    remote(pd_out.at[s], p_in.at[j], pd_send, p_recv.at[j], (row - 1, s)).start()
-
-            inner = lax.dot_general(y, v_ref[q], NT, preferred_element_type=jnp.float32)
+                    remote(w2_out, w2_in, pd_send, p_recv.at[whole], (row - 1, s)).start()
+                for peer in peers:
+                    remote(w2_out, w2_in, du_send, x_recv, (row, peer)).start()
+                w2_in[...] = w2_out[...]
+
+            inner = jnp.dot(y, vt_ref[q], preferred_element_type=jnp.float32)
             keep = lax.broadcasted_iota(jnp.int32, (nrhs, rank_max), 1) < rank_ref[q]
             inner = jnp.where(keep, inner, 0.0).astype(jnp.bfloat16)
             p = jnp.dot(inner, u_ref[q], preferred_element_type=jnp.float32)
@@ -540,15 +550,28 @@
                 remote(p_out.at[q, peer], p_in.at[j], p_send.at[q], p_recv.at[j], (row, peer)).start()
             p_in[j] = p_out[q, col]
 
+    def products():
+        fold_with(v_in, v_recv, fold)
+        factor = fold[...].astype(jnp.bfloat16)
+        shared_wait(u_in, u_recv, prev_home)
+        shared_wait(l_in, k_recv, mine_home)
+        a_out[0] = jnp.dot(u_in[...].astype(jnp.bfloat16), factor, preferred_element_type=jnp.float32)
+        a_out[1] = jnp.dot(l_in[...].astype(jnp.bfloat16), factor, preferred_element_type=jnp.float32)
+        shared_wait(l2_in, du_recv, whole_home)
+        a_out[2] = jnp.dot(l2_in[...].astype(jnp.bfloat16), factor, preferred_element_type=jnp.float32)
+        for k in range(3):
+            for s in range(n_col):
+                remote(a_out.at[k], a_in.at[k, col], a_send, a_recv, (row + 1, s)).start()
+
+    @pl.when(relays_late)
+    def _():
+        products()
+        relay(v_out, v_in, v_recv, row - 1, prev_home)
+
     @pl.when(takes | takes_whole)
     def _():
         remote(d_in, d_in, d_send, d_recv, (row - 1, col)).wait_recv()
-        d_tile[...] = d_in[...].astype(jnp.bfloat16)
-
-    @pl.when(takes_whole)
-    def _():
-        remote(du_in, du_in, du_send, du_recv, (row - 1, col)).wait_recv()
-        du_tile[...] = du_in[...].astype(jnp.bfloat16)
+        d_tile[...] = d_in[...].T.astype(jnp.bfloat16)
 
     @pl.when(is_end & (col != far_home))
     def _():
@@ -572,7 +595,7 @@
         tail = tail_of(c)
         slot = (ahead - 1) // n_col
         home = (ahead - 1) % n_col
-        return remote(hy_out.at[:, tail], y_in.at[slot, c, :, tail], y_send.at[end], y_recv.at[slot, c], (end, home))
+        return remote(hy_out.at[:, tail], y_in.at[slot, c, :, tail], y_send.at[0], y_recv.at[slot, c], (end, home))
 
     @pl.when(is_ahead)
     def _():
@@ -616,17 +639,7 @@
     for q in range(per_col):
         long_step(q, is_ahead & (q * n_col + col == row - 2))
 
-    @pl.when(is_even_end)
-    def _():
-        fold_with(v_in, v_recv, fold)
-        factor = fold[...].astype(jnp.bfloat16)
-        shared_wait(u_in, u_recv, prev_home)
-        shared_wait(l_in, k_recv, mine_home)
-        a_out[0] = jnp.dot(u_in[...].astype(jnp.bfloat16), factor, preferred_element_type=jnp.float32)
-        a_out[1] = jnp.dot(l_in[...].astype(jnp.bfloat16), factor, preferred_element_type=jnp.float32)
-        for k in range(2):
-            for s in range(n_col):
-                remote(a_out.at[k], a_in.at[k, col], a_send, a_recv, (row + 1, s)).start()
+    pl.when(is_even_end & jnp.logical_not(relays_late))(products)
 
     @pl.when(feeds & jnp.logical_not(is_even_end))
     def _():
@@ -656,7 +669,7 @@
     @pl.when(is_end)
     def _():
         remote(a_in, a_in, a_send, a_recv, (row - 1, 0)).wait_recv()
-        for k in range(2):
+        for k in range(3):
             total = a_in[k, 0]
             for s in range(1, n_col):
                 total = total + a_in[k, s]
@@ -686,11 +699,6 @@
 
     @pl.when(is_even_end)
     def _():
-        remote(p_in.at[whole], p_in.at[whole], p_send.at[0], p_recv.at[whole], (row + 1, whole_home)).wait_recv()
-        base[...] -= p_in[whole]
-
-    @pl.when(is_even_end)
-    def _():
         w_out[...] = jnp.dot(base[...].astype(jnp.bfloat16), fold[...].astype(jnp.bfloat16), preferred_element_type=jnp.float32)
         send_w(w_out, w_in, w_send, w_recv, row + 1)
 
@@ -701,6 +709,14 @@
             shared_wait(l_in, k_recv, mine_home)
 
         l_part = l_in[...].astype(jnp.bfloat16)
+
+        @pl.when(is_even_end)
+        def _():
+            remote(w2_in, w2_in, pd_send, p_recv.at[whole], (row + 1, whole_home)).wait_recv()
+            base[...] -= jnp.dot(
+                w2_in[...].astype(jnp.bfloat16), l2_in[...].astype(jnp.bfloat16), preferred_element_type=jnp.float32
+            )
+
         remote(wl_in, wl_in, wl_send, wl_recv, (row + 1, mine_home)).wait_recv()
         base[...] -= jnp.dot(wl_in[...].astype(jnp.bfloat16), l_part, preferred_element_type=jnp.float32)
 
@@ -736,7 +752,12 @@
         def _():
             remote(wl_in, wl_in, wp_send, wl_recv, (row, their_home)).wait_recv()
 
+        @pl.when(jnp.logical_not(takes_whole))
+        def _():
+            remote(w2_in, w2_in, du_send, x_recv, (row, whole_home)).wait_recv()
+
         inner = wait_w(w_in, w_send, w_recv, row - 1)
+        inner -= jnp.dot(w2_in[...].astype(jnp.bfloat16), a_sum[2], preferred_element_type=jnp.float32)
         inner -= jnp.dot(wl_in[...].astype(jnp.bfloat16), a_sum[1], preferred_element_type=jnp.float32)
         late = wait_w(wx_in, wx_send, wx_recv, row - 2)
         base[...] -= jnp.dot(late.astype(jnp.bfloat16), t_part, preferred_element_type=jnp.float32)
@@ -756,6 +777,7 @@
 
         @pl.when(is_ahead)
         def _():
+            send_w(w_out, w_in, w_send, w_recv, row + 1)
             send_w(w_out, we_in, we_send, we_recv, row + 2)
             wx_out[...] = jnp.dot(reduced, fold_x[...].astype(jnp.bfloat16), preferred_element_type=jnp.float32)
             send_w(wx_out, wx_in, wx_send, wx_recv, row + 2)
@@ -764,7 +786,7 @@
         def _():
             send_w(w_out, hw_in, w_send, du_recv, row + 2)
 
-        @pl.when(jnp.logical_not(before))
+        @pl.when(jnp.logical_not(before | is_ahead))
         def _():
             send_w(w_out, w_in, w_send, w_recv, row + 1)
 
@@ -777,7 +799,7 @@
     def near_copy(i, c):
         tail = tail_of(c)
         return remote(
-            y_row.at[c, :, tail], y_in.at[own_slot, c, :, tail], y_send.at[i], y_recv.at[own_slot, c], (i, own_home)
+            y_row.at[c, :, tail], y_in.at[own_slot, c, :, tail], y_send.at[lax.rem(i - row - 1, y_sends)], y_recv.at[own_slot, c], (i, own_home)
         )
 
     def send_y(i, carry):
@@ -860,11 +882,12 @@
     @pl.when(hands_whole)
     def _():
         remote(d_out, d_in, d_send, d_recv, (row + 1, col)).wait_send()
-        remote(du_out, du_in, du_send, du_recv, (row + 1, col)).wait_send()
+        share_done(l_out)
 
     @pl.when(takes_whole)
     def _():
-        remote(pd_out, pd_out, pd_send, p_recv.at[0], (row - 1, 0)).wait_send()
+        remote(w_in, w_in, pd_send, p_recv.at[0], (row - 1, 0)).wait_send()
+        remote(w_in.at[others], w_in.at[others], du_send, x_recv, (row, peers[0])).wait_send()
 
     @pl.when(gives)
     def _():
@@ -903,7 +926,7 @@
     y_all[...] = y
 
     def far_copy(i):
-        return remote(y_all, y_in.at[own_slot, 0], y_send.at[i], y_recv.at[own_slot, 0], (i, col))
+        return remote(y_all, y_in.at[own_slot, 0], y_send.at[lax.rem(i - row - 1, y_sends)], y_recv.at[own_slot, 0], (i, col))
 
     def send_far(i, carry):
         far_copy(i).start()
@@ -980,19 +1003,19 @@
             *tile_set,
             f32(rank_max, width),
             f32(rank_max, width),
-            bf16(rank_max, width),
-            f32(rank_max, width),
-            f32(rank_max, width),
-            bf16(rank_max, width),
-            f32(n_col, nrhs, piece),
+            bf16(width, rank_max),
+            bf16(per_col, width, rank_max),
+            f32(rank_max, piece),
+            f32(nrhs, rank_max),
+            f32(nrhs, rank_max),
             f32(n_col, rank_max, piece),
             f32(rank_max, piece),
             f32(nrhs, rank_max),
             f32(nrhs, rank_max),
             f32(n_col, nrhs, rank_max),
-            f32(2, rank_max, rank_max),
-            f32(2, n_col, rank_max, rank_max),
-            bf16(2, rank_max, rank_max),
+            f32(3, rank_max, rank_max),
+            f32(3, n_col, rank_max, rank_max),
+            bf16(3, rank_max, rank_max),
             f32(rank_max, piece),
             f32(rank_max, piece),
             f32(piece, rank_max),
@@ -1007,10 +1030,10 @@
             f32(n_col, nrhs, rank_max),
             f32(nrhs, width),
             dma((5,)),
-            dma((n_row,)),
+            dma((max(NEAR + 1, n_row - NEAR - 1),)),
             dma((per_col, n_col)),
             dma((per_col,)),
-            dma((n_row,)),
+            dma((n_row - 3,)),
             dma, dma((n_col,)), dma, dma,
             dma((n_col,)),
             dma, dma, dma, dma, dma,

time: 30.2 us -> 29.4 us (0.974)
  Pallas kernels: 28.3 us -> 27.4 us
    pallas_call x1, Pallas kernels: 28.3 us -> 27.4 us  [local(): pl.pallas_call(functools.partial(kernel, n_row, n_col), out_shape=(pltpu....]
where the time goes in v6:
time: 29.4 us; the launch traced here: 29.2 us
  Pallas kernels  27.4 us (93%)
  local copies, waits for them, and re-layouts  1.12 us (4%)
  between operations  0.64 us (2%)
    pallas_call x1, Pallas kernels, local(): pl.pallas_call(functools.partial(kernel, n_row, n_col), out_shape=(pltpu....  27.4 us
    unnamed x2, local copies, waits for them, and re-layouts  1.12 us

profile of v6, /device:TPU:25, one launch (start us, length us, event | category | flops | bytes accessed | tf_op | source)
XLA Modules:
  0.0 29.2 jit_solution(11116010637310570194)
XLA Ops:
  0.6 27.4 %forward_solve.1 = (f32[1,1,4,1024]{3,2,1,0:T(4,128)S(1)}, f32[1,1,4]{2,1,0:T(1,128)S(1)}) custom-call(f32[1,1,4,1024]{3,2,1,0:T(4,128)} %rhs_hbm.1, bf16[1,1,256,1024]{3,2,1,0:T(8,128)(2,1)} %inv_hbm.1, bf16[1,1,2,1,128,1024]{5,4,3,2,1,0:T(8,128)(2,1)} %u_hbm.1, bf16[1,1,2,1,128,1024]{5,4,3,2,1,0:T(8,128)(2,1)} %v_hbm.1, s32[2]{0:T(128)} %bitcast.1), custom_call_target="tpu_custom_call" | custom-call | tf_op jit(solution)/shard_map/forward_solve/pallas_call | solution.py:980
  28.0 0.6 %copy.9 = f32[1,1,4,1024]{3,2,1,0:T(4,128)} copy(f32[1,1,4,1024]{3,2,1,0:T(4,128)S(1)} %get-tuple-element.2) | data formatting | bytes 32768
  28.6 0.5 %copy.10 = f32[1,1,4]{2,1,0:T(1,128)} copy(f32[1,1,4]{2,1,0:T(1,128)S(1)} %get-tuple-element.3) | data formatting | bytes 32

commit v7 on v6

--- a/solution.py
+++ b/solution.py
@@ -30,15 +30,15 @@
     rhs_hbm, inv_hbm, u_hbm, v_hbm, rank_hbm,
     white_ref, lik_ref,
     rhs_ref, inv_ref, u_ref, v_ref, rank_ref,
-    y_in, p_out, p_in, y_row, logs, base, y_full, y_all,
+    y_in, p_out, p_in, y_row, logs, base, y_full, y_all, tally,
     v_out, v_in, u_out, u_in, fold, w_out, w_in,
     x_out, x_in, t_out, t_in, fold_x, wx_out, wx_in,
     d_out, d_in, d_tile, vt_ref, l2_in, w2_out, w2_in, l_out, l_in, wl_out, wl_in, we_in,
     a_out, a_in, a_sum,
     hl_in, hu_in, hf_in, hv_out, hv_in, hv_tile, hb_out, hb_in, hz_out, hz_in, hw_out, hw_in, hy_out,
     in_sem, y_send, y_recv, p_send, p_recv, o_send, o_recv, l_send, l_recv,
-    v_send, v_recv, u_send, u_recv, w_send, w_recv, m_recv, f_send, e_send, ready,
-    x_recv, t_recv, k_recv, d_send, d_recv, du_send, du_recv, pd_send, wl_send, wl_recv, wp_send,
+    v_send, v_recv, u_send, u_recv, w_send, w_recv, m_recv, f_send, e_send, ready, ready_far, pass_send,
+    x_recv, t_recv, k_recv, d_send, d_recv, du_recv, wl_send, wl_recv, wp_send,
     we_send, we_recv, wx_send, wx_recv, a_send, a_recv,
 ):
     row = lax.axis_index("row")
@@ -48,7 +48,7 @@
     piece = width // n_col
     half = n_col // 2
     y_sends = y_send.shape[0]
-    some = max(n_col // 4, 1)
+    some = half
     peers = [lax.rem(col + k, n_col) for k in range(1, n_col)]
     others = pl.ds(0, n_col - 1)
     own_slot = row // n_col
@@ -63,7 +63,7 @@
         return count - jnp.where(handed, 1, 0) - jnp.where(i >= even_end, 1, 0)
 
     def near_of(i):
-        return NEAR + jnp.where(i >= 2, 1, 0)
+        return jnp.where(i == 0, 1, NEAR + jnp.where(i >= 2, 1, 0))
 
     copies = [
         pltpu.make_async_copy(v_hbm.at[0, 0, :, 0], v_ref, in_sem.at[0]),
@@ -91,6 +91,43 @@
     by_col(lambda c: inverse_copy(c).start())
     for copy in copies[3:]:
         copy.start()
+    barrier = pltpu.get_barrier_semaphore()
+
+    def signal(sem, i, s):
+        pl.semaphore_signal(sem, inc=1, device_id=(i, s), device_id_type=MESH)
+
+    for peer in peers:
+        signal(barrier, row, peer)
+
+    def set_base():
+        for cc in range(n_col):
+
+            @pl.when(col == cc)
+            def _():
+                base[...] = rhs_ref[:, cc * piece:(cc + 1) * piece]
+
+    def own_part(c, reduced):
+        tail = tail_of(c)
+        y_row[c, :, tail] = jnp.dot(reduced, inv_ref[:, tail], preferred_element_type=jnp.float32)
+
+    def near_copy(i, c):
+        tail = tail_of(c)
+        sem = y_send.at[lax.rem(i - row - 1, y_sends)]
+        return remote(y_row.at[c, :, tail], y_in.at[own_slot, c, :, tail], sem, y_recv.at[own_slot], (i, own_home))
+
+    first = row == 0
+
+    @pl.when(first)
+    def _():
+        for s in range(n_col):
+            signal(barrier, 1, s)
+        copies[3].wait()
+        by_col(lambda c: inverse_copy(c).wait())
+        set_base()
+        reduced = base[...].astype(jnp.bfloat16)
+        by_col(lambda c: own_part(c, reduced))
+        pl.semaphore_wait(barrier, 2 * n_col - 1)
+        by_col(lambda c: near_copy(1, c).start())
 
     for s in range(1, n_col):
         start = s * piece // 128 * 128
@@ -109,12 +146,8 @@
     before = row == ahead - 2
     long_count = longs_of(row)
     near_end = jnp.minimum(row + near_of(row) + 1, n_row)
-    relays = col == own_home
-
-    barrier = pltpu.get_barrier_semaphore()
-
-    def signal(sem, i, s):
-        pl.semaphore_signal(sem, inc=1, device_id=(i, s), device_id_type=MESH)
+    relays = (col == own_home) & (row > 0)
+    passes = (row == 1) & (col == 0)
 
     def row_of(i, cond, act):
         @pl.when(cond)
@@ -125,7 +158,7 @@
         return jnp.where(cond, n_col, 0)
 
     def above(act):
-        yield row + 1, row_of(row + 1, row < end, act)
+        yield row + 1, row_of(row + 1, (row > 0) & (row < end), act)
         for d in range(2, NEAR + 2):
             wide = (is_ahead | before) if d == 2 else jnp.bool_(False)
             one = (row + d < n_row) & (d <= near_of(row)) & jnp.logical_not(wide)
@@ -138,7 +171,7 @@
             if d == 2:
                 yield row + d, row_of(row + d, wide, act)
 
-    def below(act):
+    def below(act, act_far=None):
         row_of(row - 1, row > 0, act)
         count = jnp.where(row > 0, n_col, 0)
         for d in range(2, NEAR + 2):
@@ -150,9 +183,16 @@
             j = q * n_col + col
             far = j < row - near_of(j)
 
-            @pl.when(far)
-            def _():
-                act(j, col)
+            source = jnp.where(j == 0, 1, j)
+            soon = (j == 0) & (row <= 3)
+
+            @pl.when(far & soon)
+            def _():
+                act(source, col)
+
+            @pl.when(far & jnp.logical_not(soon))
+            def _():
+                (act_far or act)(source, col)
 
             count += jnp.where(far, 1, 0)
         return count
@@ -160,20 +200,18 @@
     def at_once(low, high):
         return (low == 0) & (high == 1)
 
-    for peer in peers:
-        signal(barrier, row, peer)
     greeted = jnp.int32(n_col - 1)
     answers = jnp.int32(0)
     for i, count in above(lambda i, s: signal(barrier, i, s)):
-        quick = at_once(row, i)
-        greeted += jnp.where(quick, count, 0)
-        answers += jnp.where(quick, 0, count)
+        answers += count
 
     def greet_far(i, count):
         signal(barrier, i, col)
         return count + 1
 
-    answers = lax.fori_loop(jnp.where(relays, near_end, n_row), n_row, greet_far, answers)
+    far_answers = lax.fori_loop(jnp.where(relays, near_end, n_row), n_row, greet_far, jnp.int32(0))
+    far_answers = lax.fori_loop(jnp.where(passes, 4, n_row), n_row, greet_far, far_answers)
+    answers = lax.fori_loop(jnp.where(passes, 2, n_row), jnp.where(passes, 4, n_row), greet_far, answers)
 
     def greet_quick(i, s):
         @pl.when(at_once(i, row))
@@ -245,8 +283,11 @@
         cut(v_ref[far_slot].astype(jnp.float32), x_out)
         cut(masked_u(far_slot), t_out)
 
-    pl.semaphore_wait(barrier, greeted)
-    below(answer)
+    @pl.when(row > 0)
+    def _():
+        pl.semaphore_wait(barrier, greeted)
+
+    below(answer, lambda i, s: signal(ready_far, i, s))
 
     def by_way(home, s, cc):
         across = n_col - 1 - home
@@ -268,6 +309,13 @@
         return (across > home) & (across == s)
 
     def spread(out, into, recv, target, home, cross):
+        for s in range(n_col):
+            for cc in range(s, min(s + some, n_col)):
+
+                @pl.when(cross & is_split(home, s))
+                def _():
+                    remote(out.at[cc], out.at[cc], v_send.at[s], m_recv.at[cc], (row, s)).start()
+
         for s in range(n_col):
             if s > 0:
 
@@ -286,19 +334,12 @@
 
                 @pl.when(jnp.logical_not(way | later | gone))
                 def _():
-                    remote(out.at[cc], into.at[cc], v_send.at[s], recv, (target, s)).start()
-
+                    remote(out.at[cc], into.at[cc], v_send.at[s], recv.at[cc], (target, s)).start()
+
+    def spread_late(out, into, recv, target, home):
         for s in range(n_col):
-            for cc in range(s, min(s + some, n_col)):
-
-                @pl.when(cross & is_split(home, s))
-                def _():
-                    remote(out.at[cc], out.at[cc], v_send.at[s], m_recv.at[cc], (row, s)).start()
-
-    def spread_late(out, into, recv, target, home):
-        for s in range(n_col - 1):
-
-            @pl.when(split_row(home) & (home == s + 1))
+
+            @pl.when(split_row(home) & (n_col - home == s))
             def _():
                 part = pl.ds(s, n_col - s)
                 remote(out.at[part], out.at[part], v_send.at[s], m_recv.at[0], (row, s)).wait_send()
@@ -308,13 +349,13 @@
 
                 @pl.when(is_late(home, s, cc))
                 def _():
-                    remote(out.at[cc], into.at[cc], v_send.at[s], recv, (target, s)).start()
+                    remote(out.at[cc], into.at[cc], v_send.at[s], recv.at[cc], (target, s)).start()
 
     def spread_done(out, home, cross):
         for s in range(n_col):
             part = pl.ds(s, n_col - s)
             gone = cross & joined(home, s)
-            gone = gone | (cross & split_row(home) & (home == s + 1))
+            gone = gone | (cross & split_row(home) & (n_col - home == s))
             more = (cross & joined(home, s - 1)) if s > 0 else jnp.bool_(False)
 
             @pl.when(jnp.logical_not(gone | more))
@@ -335,17 +376,22 @@
         part = jnp.where(across < home, across == col, col < home)
         share_of = jnp.where(across < home, some, half)
         stop = jnp.where(part, jnp.minimum(col + share_of, n_col), n_col)
+        stop = jnp.where(joined(home, col), col + 1, stop)
 
         def forward(cc, carry):
             remote(out.at[cc], out.at[cc], v_send.at[0], m_recv.at[cc], (row, home)).wait_recv()
 
             @pl.when(cc >= col)
             def _():
-                remote(out.at[cc], into.at[cc], f_send, recv, (target, col)).start()
-
-            @pl.when(more)
+                remote(out.at[cc], into.at[cc], f_send, recv.at[cc], (target, col)).start()
+
+            @pl.when(more & (cc == across))
             def _():
                 remote(out.at[cc], out.at[cc], e_send, m_recv.at[cc], (row, across)).start()
+
+            @pl.when(more & (cc > across))
+            def _():
+                remote(out.at[cc], into.at[cc], e_send, recv.at[cc], (target, across)).start()
 
             return carry
 
@@ -357,28 +403,37 @@
             here = col == cc
             half_way = jnp.where(across < home, across == cc, cc < home)
 
-            @pl.when(here & jnp.logical_not(half_way))
+            @pl.when(here & joined(home, cc))
+            def _():
+                remote(out.at[cc], out.at[cc], f_send, v_recv.at[0], (row, home)).wait_send()
+
+            @pl.when(here & jnp.logical_not(half_way | joined(home, cc)))
             def _():
                 part = pl.ds(cc, n_col - cc)
-                remote(out.at[part], out.at[part], f_send, v_recv, (row, home)).wait_send()
+                remote(out.at[part], out.at[part], f_send, v_recv.at[0], (row, home)).wait_send()
 
             for count, cond in ((some, across < home), (half, across > home)):
                 few = pl.ds(cc, min(count, n_col - cc))
 
                 @pl.when(here & half_way & cond)
                 def _():
-                    remote(out.at[few], out.at[few], f_send, v_recv, (row, home)).wait_send()
+                    remote(out.at[few], out.at[few], f_send, v_recv.at[0], (row, home)).wait_send()
 
             if cc > 0:
 
                 @pl.when((col == cc) & joined(home, cc - 1))
                 def _():
                     part = pl.ds(cc - 1, n_col - cc + 1)
-                    remote(out.at[part], out.at[part], e_send, v_recv, (row, home)).wait_send()
+                    remote(out.at[part], out.at[part], e_send, v_recv.at[0], (row, home)).wait_send()
 
     def share(out, into, recv):
-        for peer in peers:
-            remote(out.at[peer], into, u_send, recv, (row, peer)).start()
+        for k in range(n_col):
+            peer = lax.rem(2 * n_col - 1 - col + k, n_col)
+
+            @pl.when(peer != col)
+            def _():
+                remote(out.at[peer], into, u_send, recv, (row, peer)).start()
+
         into[...] = out[col]
 
     def share_done(out):
@@ -391,9 +446,17 @@
 
     early_l = (row < FIRST_SHORT) | is_even_end
 
-    @pl.when(hands & early_l)
-    def _():
-        share(l_out, l_in, k_recv)
+    opposite = n_col - 1 - col
+
+    @pl.when(hands)
+    def _():
+        for peer in peers:
+
+            @pl.when(early_l | (peer != opposite))
+            def _():
+                remote(l_out.at[peer], l_in, u_send, k_recv, (row, peer)).start()
+
+        l_in[...] = l_out[col]
 
     @pl.when(hands_whole)
     def _():
@@ -425,8 +488,11 @@
     def _():
         relay(v_out, v_in, v_recv, row - 1, prev_home)
 
-    by_col(lambda c: inverse_copy(c).wait())
-    copies[3].wait()
+    @pl.when(row > 0)
+    def _():
+        by_col(lambda c: inverse_copy(c).wait())
+        copies[3].wait()
+
 
     def lend(src, dst, send, recv):
         return remote(src, dst, send, recv, (row + 1, col))
@@ -440,11 +506,7 @@
 
     pl.when(lent)(functools.partial(by_col, lend_tail))
 
-    for cc in range(n_col):
-
-        @pl.when(col == cc)
-        def _():
-            base[...] = rhs_ref[:, cc * piece:(cc + 1) * piece]
+    pl.when(row > 0)(set_base)
 
     def log_part():
         for cc in range(n_col):
@@ -473,19 +535,21 @@
     def _():
         spread_late(v_out, v_in, v_recv, row - 1, prev_home)
 
+    @pl.when(gives & crosses & jnp.logical_not(is_even_end))
+    def _():
+        share(u_out, u_in, u_recv)
+
+    @pl.when(hands & jnp.logical_not(early_l))
+    def _():
+        remote(l_out.at[opposite], l_in, u_send, k_recv, (row, opposite)).start()
+
     def fold_with(into, recv, target):
         target[...] = jnp.zeros_like(target)
         for cc in range(n_col):
-            part = pl.ds(cc, n_col - cc)
-
-            @pl.when(col == cc)
-            def _():
-                remote(into.at[part], into.at[part], f_send, recv, (row, cc)).wait_recv()
-
-        for cc in range(n_col):
 
             @pl.when(col <= cc)
             def _():
+                remote(into.at[cc], into.at[cc], f_send, recv.at[cc], (row, cc)).wait_recv()
                 target[...] += lax.dot_general(
                     inv_ref[:, cc * piece:(cc + 1) * piece],
                     into[cc].astype(jnp.bfloat16),
@@ -502,9 +566,7 @@
 
             @pl.when(near)
             def _():
-                for s in range(n_col):
-                    part = y_in.at[q, s, :, tail_of(s)]
-                    remote(part, part, y_send.at[0], y_recv.at[q, s], (j, col)).wait_recv()
+                remote(tally, tally, y_send.at[0], y_recv.at[q], (j, col)).wait_recv()
                 y = y_in[q, 0]
                 for s in range(1, n_col):
                     y = y + y_in[q, s]
@@ -512,7 +574,7 @@
 
             @pl.when(jnp.logical_not(near))
             def _():
-                remote(y_in.at[q, 0], y_in.at[q, 0], y_send.at[0], y_recv.at[q, 0], (j, col)).wait_recv()
+                remote(y_in.at[q, 0], y_in.at[q, 0], y_send.at[0], y_recv.at[q], (j, col)).wait_recv()
                 y_full[...] = y_in[q, 0]
 
             y = y_full[...].astype(jnp.bfloat16)
@@ -535,9 +597,9 @@
             def _():
                 w2_out[...] = jnp.dot(y, d_tile[...], preferred_element_type=jnp.float32)
                 for s in range(n_col):
-                    remote(w2_out, w2_in, pd_send, p_recv.at[whole], (row - 1, s)).start()
+                    remote(w2_out, w2_in, wl_send, p_recv.at[whole], (row - 1, s)).start()
                 for peer in peers:
-                    remote(w2_out, w2_in, du_send, x_recv, (row, peer)).start()
+                    remote(w2_out, w2_in, wp_send, x_recv.at[0], (row, peer)).start()
                 w2_in[...] = w2_out[...]
 
             inner = jnp.dot(y, vt_ref[q], preferred_element_type=jnp.float32)
@@ -580,6 +642,15 @@
     for q in range(per_col):
         long_step(q, jnp.logical_not(is_ahead & (q * n_col + col == row - 2)))
 
+    def pass_on(i, carry):
+        remote(y_full, y_in.at[0, 0], pass_send, y_recv.at[0], (i, 0)).start()
+        return carry
+
+    @pl.when(passes)
+    def _():
+        pl.semaphore_wait(ready, answers)
+        lax.fori_loop(2, 4, pass_on, 0)
+
     def send_w(out, into, send, recv, i):
         for s in range(n_col):
             remote(out, into.at[col], send, recv, (i, s)).start()
@@ -595,7 +666,7 @@
         tail = tail_of(c)
         slot = (ahead - 1) // n_col
         home = (ahead - 1) % n_col
-        return remote(hy_out.at[:, tail], y_in.at[slot, c, :, tail], y_send.at[0], y_recv.at[slot, c], (end, home))
+        return remote(hy_out.at[:, tail], y_in.at[slot, c, :, tail], y_send.at[0], y_recv.at[slot], (end, home))
 
     @pl.when(is_ahead)
     def _():
@@ -634,7 +705,7 @@
 
         by_col(borrowed_part)
         hz_out[...] = part.astype(jnp.float32)
-        remote(hz_out, hz_in, pd_send, du_recv, back).start()
+        remote(hz_out, hz_in, wl_send, du_recv, back).start()
 
     for q in range(per_col):
         long_step(q, is_ahead & (q * n_col + col == row - 2))
@@ -648,14 +719,6 @@
         @pl.when(lent)
         def _():
             lend(fold, hf_in, wx_send, we_recv).start()
-
-    @pl.when(gives & crosses & jnp.logical_not(is_even_end))
-    def _():
-        share(u_out, u_in, u_recv)
-
-    @pl.when(hands & jnp.logical_not(early_l))
-    def _():
-        share(l_out, l_in, k_recv)
 
     @pl.when(gives_far)
     def _():
@@ -694,7 +757,7 @@
         lend(l_in, hl_in, a_send, k_recv).start()
         shared_wait(u_in, u_recv, prev_home)
         lend(u_in, hu_in, we_send, a_recv).start()
-        remote(hz_in, hz_in, pd_send, du_recv, (row + 1, col)).wait_recv()
+        remote(hz_in, hz_in, wl_send, du_recv, (row + 1, col)).wait_recv()
         base[...] = hz_in[...]
 
     @pl.when(is_even_end)
@@ -712,7 +775,7 @@
 
         @pl.when(is_even_end)
         def _():
-            remote(w2_in, w2_in, pd_send, p_recv.at[whole], (row + 1, whole_home)).wait_recv()
+            remote(w2_in, w2_in, wl_send, p_recv.at[whole], (row + 1, whole_home)).wait_recv()
             base[...] -= jnp.dot(
                 w2_in[...].astype(jnp.bfloat16), l2_in[...].astype(jnp.bfloat16), preferred_element_type=jnp.float32
             )
@@ -754,7 +817,7 @@
 
         @pl.when(jnp.logical_not(takes_whole))
         def _():
-            remote(w2_in, w2_in, du_send, x_recv, (row, whole_home)).wait_recv()
+            remote(w2_in, w2_in, wp_send, x_recv.at[0], (row, whole_home)).wait_recv()
 
         inner = wait_w(w_in, w_send, w_recv, row - 1)
         inner -= jnp.dot(w2_in[...].astype(jnp.bfloat16), a_sum[2], preferred_element_type=jnp.float32)
@@ -767,7 +830,7 @@
 
     reduced = base[...].astype(jnp.bfloat16)
 
-    @pl.when(jnp.logical_not(even | is_ahead) & (answers > 0))
+    @pl.when(jnp.logical_not(even | is_ahead | passes) & (answers > 0))
     def _():
         pl.semaphore_wait(ready, answers)
 
@@ -790,17 +853,9 @@
         def _():
             send_w(w_out, w_in, w_send, w_recv, row + 1)
 
-    def own_part(c):
-        tail = tail_of(c)
-        y_row[c, :, tail] = jnp.dot(reduced, inv_ref[:, tail], preferred_element_type=jnp.float32)
-
-    by_col(own_part)
-
-    def near_copy(i, c):
-        tail = tail_of(c)
-        return remote(
-            y_row.at[c, :, tail], y_in.at[own_slot, c, :, tail], y_send.at[lax.rem(i - row - 1, y_sends)], y_recv.at[own_slot, c], (i, own_home)
-        )
+    @pl.when(row > 0)
+    def _():
+        by_col(lambda c: own_part(c, reduced))
 
     def send_y(i, carry):
         @pl.when((row < longs_of(i)) & jnp.logical_not(lent))
@@ -811,18 +866,15 @@
 
     def own_copy(c, peer):
         part = y_row.at[c, :, tail_of(c)]
-        return remote(part, part, o_send, o_recv.at[c], (row, peer))
-
-    first = row == 0
-    lax.fori_loop(row + 1, jnp.where(first, 2, near_end), send_y, 0)
+        return remote(part, part, o_send, o_recv, (row, peer))
+
+    lax.fori_loop(row + 1, jnp.where(first, 0, near_end), send_y, 0)
     for peer in peers:
         by_col(lambda c: own_copy(c, peer).start())
 
     @pl.when(first)
     def _():
         log_part()
-        pl.semaphore_wait(ready, answers)
-        lax.fori_loop(2, near_end, send_y, 0)
 
     remote(logs.at[others], logs.at[others], l_send, l_recv, (row, peers[0])).wait()
     log_sum = logs[0]
@@ -856,7 +908,7 @@
         part = w_in.at[others]
         remote(part, part, a_send, w_recv, (row, peers[0])).wait_send()
         by_col(lambda c: borrowed_y(c).wait_send())
-        remote(hz_out, hz_in, pd_send, du_recv, (row - 1, col)).wait_send()
+        remote(hz_out, hz_in, wl_send, du_recv, (row - 1, col)).wait_send()
         remote(w_in, w_in, we_send, we_recv, (row + 2, 0)).wait_send()
         remote(w_in, w_in, wx_send, wx_recv, (row + 2, 0)).wait_send()
 
@@ -886,8 +938,8 @@
 
     @pl.when(takes_whole)
     def _():
-        remote(w_in, w_in, pd_send, p_recv.at[0], (row - 1, 0)).wait_send()
-        remote(w_in.at[others], w_in.at[others], du_send, x_recv, (row, peers[0])).wait_send()
+        remote(w_in, w_in, wl_send, p_recv.at[0], (row - 1, 0)).wait_send()
+        remote(w_in.at[others], w_in.at[others], wp_send, x_recv.at[0], (row, peers[0])).wait_send()
 
     @pl.when(gives)
     def _():
@@ -914,23 +966,32 @@
             part = p_out.at[q, others]
             remote(part, part, p_send.at[q], p_recv.at[0], (row, peers[0])).wait_send()
 
-    for s in range(n_col):
-
-        @pl.when(col != s)
-        def _():
-            own_copy(s, peers[0]).wait_recv()
-
+    def wait_others(c):
+        part = tally.at[pl.ds(0, tally.shape[0] - tail_of(c).size // 128)]
+        remote(part, part, o_send, o_recv, (row, peers[0])).wait_recv()
+
+    by_col(wait_others)
     y = y_row[0]
     for s in range(1, n_col):
         y = y + y_row[s]
     y_all[...] = y
 
     def far_copy(i):
-        return remote(y_all, y_in.at[own_slot, 0], y_send.at[lax.rem(i - row - 1, y_sends)], y_recv.at[own_slot, 0], (i, col))
+        return remote(y_all, y_in.at[own_slot, 0], y_send.at[lax.rem(i - row - 1, y_sends)], y_recv.at[own_slot], (i, col))
 
     def send_far(i, carry):
         far_copy(i).start()
         return carry
+
+    @pl.when(far_answers > 0)
+    def _():
+        pl.semaphore_wait(ready_far, far_answers)
+
+    @pl.when(passes)
+    def _():
+        lax.fori_loop(4, n_row, pass_on, 0)
+        part = y_in.at[:, pl.ds(0, (n_row - 2) // per_col)]
+        remote(part, part, pass_send, y_recv.at[0], (2, 0)).wait_send()
 
     lax.fori_loop(jnp.where(relays, near_end, n_row), n_row, send_far, 0)
     white_ref[0, 0] = y
@@ -949,7 +1010,7 @@
 
     def own_left(c):
         part = y_row.at[others, :, tail_of(c)]
-        remote(part, part, o_send, o_recv.at[c], (row, peers[0])).wait_send()
+        remote(part, part, o_send, o_recv, (row, peers[0])).wait_send()
 
     by_col(own_left)
 
@@ -968,6 +1029,7 @@
     def bf16(*shape):
         return pltpu.VMEM(shape, jnp.bfloat16)
 
+    units = sum((width - c * piece // 128 * 128) // 128 for c in range(n_col))
     tile_set = [
         f32(n_col, rank_max, piece),
         f32(n_col, rank_max, piece),
@@ -999,6 +1061,7 @@
             f32(nrhs, piece),
             f32(nrhs, width),
             f32(nrhs, width),
+            f32(units, nrhs, 128),
             *tile_set,
             *tile_set,
             f32(rank_max, width),
@@ -1031,18 +1094,21 @@
             f32(nrhs, width),
             dma((5,)),
             dma((max(NEAR + 1, n_row - NEAR - 1),)),
-            dma((per_col, n_col)),
+            dma((per_col,)),
             dma((per_col,)),
             dma((n_row - 3,)),
-            dma, dma((n_col,)), dma, dma,
+            dma, dma, dma, dma,
             dma((n_col,)),
-            dma, dma, dma, dma, dma,
+            dma((n_col,)),
+            dma, dma, dma, dma,
             dma((n_col,)),
             dma, dma,
             pltpu.SemaphoreType.REGULAR,
-            dma, dma, dma, dma, dma, dma, dma, dma,
-            dma, dma, dma,
-            dma, dma, dma, dma, dma, dma,
+            pltpu.SemaphoreType.REGULAR,
+            dma,
+            dma((n_col,)),
+            dma, dma, dma, dma, dma,
+            dma, dma, dma, dma, dma, dma, dma, dma, dma,
         ],
         compiler_params=pltpu.CompilerParams(collective_id=0, has_side_effects=True),
         name="forward_solve",

time: 29.4 us -> 28.6 us (0.973)
  Pallas kernels: 27.4 us -> 26.5 us
    pallas_call x1, Pallas kernels: 27.4 us -> 26.5 us  [local(): pl.pallas_call(functools.partial(kernel, n_row, n_col), out_shape=(pltpu....]
where the time goes in v7:
time: 28.6 us; the launch traced here: 28.2 us
  Pallas kernels  26.5 us (93%)
  local copies, waits for them, and re-layouts  1.12 us (4%)
  between operations  0.64 us (2%)
    pallas_call x1, Pallas kernels, local(): pl.pallas_call(functools.partial(kernel, n_row, n_col), out_shape=(pltpu....  26.5 us
    unnamed x2, local copies, waits for them, and re-layouts  1.12 us

profile of v7, /device:TPU:25, one launch (start us, length us, event | category | flops | bytes accessed | tf_op | source)
XLA Modules:
  0.0 28.2 jit_solution(5587687983874311628)
XLA Ops:
  0.6 26.5 %forward_solve.1 = (f32[1,1,4,1024]{3,2,1,0:T(4,128)S(1)}, f32[1,1,4]{2,1,0:T(1,128)S(1)}) custom-call(f32[1,1,4,1024]{3,2,1,0:T(4,128)} %rhs_hbm.1, bf16[1,1,256,1024]{3,2,1,0:T(8,128)(2,1)} %inv_hbm.1, bf16[1,1,2,1,128,1024]{5,4,3,2,1,0:T(8,128)(2,1)} %u_hbm.1, bf16[1,1,2,1,128,1024]{5,4,3,2,1,0:T(8,128)(2,1)} %v_hbm.1, s32[2]{0:T(128)} %bitcast.1), custom_call_target="tpu_custom_call" | custom-call | tf_op jit(solution)/shard_map/forward_solve/pallas_call | solution.py:1042
  27.1 0.6 %copy.9 = f32[1,1,4,1024]{3,2,1,0:T(4,128)} copy(f32[1,1,4,1024]{3,2,1,0:T(4,128)S(1)} %get-tuple-element.2) | data formatting | bytes 32768
  27.7 0.5 %copy.10 = f32[1,1,4]{2,1,0:T(1,128)} copy(f32[1,1,4]{2,1,0:T(1,128)S(1)} %get-tuple-element.3) | data formatting | bytes 32

commit v8 on v7

--- a/solution.py
+++ b/solution.py
@@ -38,8 +38,8 @@
     hl_in, hu_in, hf_in, hv_out, hv_in, hv_tile, hb_out, hb_in, hz_out, hz_in, hw_out, hw_in, hy_out,
     in_sem, y_send, y_recv, p_send, p_recv, o_send, o_recv, l_send, l_recv,
     v_send, v_recv, u_send, u_recv, w_send, w_recv, m_recv, f_send, e_send, ready, ready_far, pass_send,
-    x_recv, t_recv, k_recv, d_send, d_recv, du_recv, wl_send, wl_recv, wp_send,
-    we_send, we_recv, wx_send, wx_recv, a_send, a_recv,
+    t_recv, k_recv, d_send, d_recv, du_recv, wl_send, wl_recv, wp_send,
+    we_send, we_recv, wx_send, wm_recv, a_send, a_recv,
 ):
     row = lax.axis_index("row")
     col = lax.axis_index("col")
@@ -291,11 +291,18 @@
 
     def by_way(home, s, cc):
         across = n_col - 1 - home
-        return (home != s) & jnp.where(across < home, (across != s) | (cc < s + some), (s > home) | (cc < s + half))
+        return (home != s) & jnp.where(
+            across < home,
+            jnp.where(across == s, cc < s + some, (home != s + 1) | (cc == s)),
+            (s > home) | (cc < s + half),
+        )
 
     def is_late(home, s, cc):
         across = n_col - 1 - home
         return (across == s) & (across < home) & (cc >= s + some)
+
+    def beside(home, s):
+        return split_row(home) & (home == s + 1) & (n_col - 1 - home != s)
 
     def split_row(home):
         return n_col - 1 - home < home
@@ -376,7 +383,7 @@
         part = jnp.where(across < home, across == col, col < home)
         share_of = jnp.where(across < home, some, half)
         stop = jnp.where(part, jnp.minimum(col + share_of, n_col), n_col)
-        stop = jnp.where(joined(home, col), col + 1, stop)
+        stop = jnp.where(joined(home, col) | beside(home, col), col + 1, stop)
 
         def forward(cc, carry):
             remote(out.at[cc], out.at[cc], v_send.at[0], m_recv.at[cc], (row, home)).wait_recv()
@@ -403,11 +410,11 @@
             here = col == cc
             half_way = jnp.where(across < home, across == cc, cc < home)
 
-            @pl.when(here & joined(home, cc))
+            @pl.when(here & (joined(home, cc) | beside(home, cc)))
             def _():
                 remote(out.at[cc], out.at[cc], f_send, v_recv.at[0], (row, home)).wait_send()
 
-            @pl.when(here & jnp.logical_not(half_way | joined(home, cc)))
+            @pl.when(here & jnp.logical_not(half_way | joined(home, cc) | beside(home, cc)))
             def _():
                 part = pl.ds(cc, n_col - cc)
                 remote(out.at[part], out.at[part], f_send, v_recv.at[0], (row, home)).wait_send()
@@ -472,7 +479,7 @@
 
     @pl.when(gives_far)
     def _():
-        spread(x_out, x_in, x_recv, row - 2, far_home, jnp.bool_(True))
+        spread(x_out, x_in, m_recv, row - 2, far_home, jnp.bool_(True))
 
     @pl.when((handed) & (answers > 0))
     def _():
@@ -498,7 +505,7 @@
         return remote(src, dst, send, recv, (row + 1, col))
 
     def lend_inverse(c):
-        return lend(hv_out.at[:, tail_of(c)], hv_in.at[:, tail_of(c)], wl_send, wx_recv)
+        return lend(hv_out.at[:, tail_of(c)], hv_in.at[:, tail_of(c)], wl_send, wm_recv)
 
     def lend_tail(c):
         hv_out[:, tail_of(c)] = inv_ref[:, tail_of(c)].astype(jnp.float32)
@@ -599,7 +606,7 @@
                 for s in range(n_col):
                     remote(w2_out, w2_in, wl_send, p_recv.at[whole], (row - 1, s)).start()
                 for peer in peers:
-                    remote(w2_out, w2_in, wp_send, x_recv.at[0], (row, peer)).start()
+                    remote(w2_out, w2_in, wp_send, k_recv, (row, peer)).start()
                 w2_in[...] = w2_out[...]
 
             inner = jnp.dot(y, vt_ref[q], preferred_element_type=jnp.float32)
@@ -637,7 +644,7 @@
 
     @pl.when(is_end & (col != far_home))
     def _():
-        relay(x_out, x_in, x_recv, row - 2, far_home)
+        relay(x_out, x_in, m_recv, row - 2, far_home)
 
     for q in range(per_col):
         long_step(q, jnp.logical_not(is_ahead & (q * n_col + col == row - 2)))
@@ -671,7 +678,7 @@
     @pl.when(is_ahead)
     def _():
         back = (row - 1, col)
-        by_col(lambda c: remote(hv_in.at[:, tail_of(c)], hv_in.at[:, tail_of(c)], wl_send, wx_recv, back).wait_recv())
+        by_col(lambda c: remote(hv_in.at[:, tail_of(c)], hv_in.at[:, tail_of(c)], wl_send, wm_recv, back).wait_recv())
         by_col(lambda c: hv_tile.__setitem__((slice(None), tail_of(c)), hv_in[:, tail_of(c)].astype(jnp.bfloat16)))
         remote(hl_in, hl_in, a_send, k_recv, back).wait_recv()
         remote(hu_in, hu_in, we_send, a_recv, back).wait_recv()
@@ -693,17 +700,17 @@
         inner = wait_w(hw_in, w_send, du_recv, row - 2)
         part -= jnp.dot(inner.astype(jnp.bfloat16), u_part, preferred_element_type=jnp.float32)
         part = part.astype(jnp.bfloat16)
+        def borrowed_part(c):
+            tail = tail_of(c)
+            hy_out[:, tail] = jnp.dot(part, hv_tile[:, tail], preferred_element_type=jnp.float32)
+            borrowed_y(c).start()
+
+        by_col(borrowed_part)
         hw_out[...] = jnp.dot(part, factor, preferred_element_type=jnp.float32)
         for peer in peers:
             remote(hw_out, w_in.at[col], a_send, w_recv, (row, peer)).start()
         w_in[col] = hw_out[...]
 
-        def borrowed_part(c):
-            tail = tail_of(c)
-            hy_out[:, tail] = jnp.dot(part, hv_tile[:, tail], preferred_element_type=jnp.float32)
-            borrowed_y(c).start()
-
-        by_col(borrowed_part)
         hz_out[...] = part.astype(jnp.float32)
         remote(hz_out, hz_in, wl_send, du_recv, back).start()
 
@@ -722,12 +729,12 @@
 
     @pl.when(gives_far)
     def _():
-        spread_late(x_out, x_in, x_recv, row - 2, far_home)
+        spread_late(x_out, x_in, m_recv, row - 2, far_home)
         share(t_out, t_in, t_recv)
 
     @pl.when(is_ahead)
     def _():
-        fold_with(x_in, x_recv, fold_x)
+        fold_with(x_in, m_recv, fold_x)
 
     @pl.when(is_end)
     def _():
@@ -817,12 +824,12 @@
 
         @pl.when(jnp.logical_not(takes_whole))
         def _():
-            remote(w2_in, w2_in, wp_send, x_recv.at[0], (row, whole_home)).wait_recv()
+            remote(w2_in, w2_in, wp_send, k_recv, (row, whole_home)).wait_recv()
 
         inner = wait_w(w_in, w_send, w_recv, row - 1)
         inner -= jnp.dot(w2_in[...].astype(jnp.bfloat16), a_sum[2], preferred_element_type=jnp.float32)
         inner -= jnp.dot(wl_in[...].astype(jnp.bfloat16), a_sum[1], preferred_element_type=jnp.float32)
-        late = wait_w(wx_in, wx_send, wx_recv, row - 2)
+        late = wait_w(wx_in, wx_send, wm_recv, row - 2)
         base[...] -= jnp.dot(late.astype(jnp.bfloat16), t_part, preferred_element_type=jnp.float32)
         late = wait_w(we_in, we_send, we_recv, row - 2)
         inner -= jnp.dot(late.astype(jnp.bfloat16), a_sum[0], preferred_element_type=jnp.float32)
@@ -843,7 +850,7 @@
             send_w(w_out, w_in, w_send, w_recv, row + 1)
             send_w(w_out, we_in, we_send, we_recv, row + 2)
             wx_out[...] = jnp.dot(reduced, fold_x[...].astype(jnp.bfloat16), preferred_element_type=jnp.float32)
-            send_w(wx_out, wx_in, wx_send, wx_recv, row + 2)
+            send_w(wx_out, wx_in, wx_send, wm_recv, row + 2)
 
         @pl.when(before)
         def _():
@@ -910,7 +917,7 @@
         by_col(lambda c: borrowed_y(c).wait_send())
         remote(hz_out, hz_in, wl_send, du_recv, (row - 1, col)).wait_send()
         remote(w_in, w_in, we_send, we_recv, (row + 2, 0)).wait_send()
-        remote(w_in, w_in, wx_send, wx_recv, (row + 2, 0)).wait_send()
+        remote(w_in, w_in, wx_send, wm_recv, (row + 2, 0)).wait_send()
 
     @pl.when(is_even_end)
     def _():
@@ -939,7 +946,7 @@
     @pl.when(takes_whole)
     def _():
         remote(w_in, w_in, wl_send, p_recv.at[0], (row - 1, 0)).wait_send()
-        remote(w_in.at[others], w_in.at[others], wp_send, x_recv.at[0], (row, peers[0])).wait_send()
+        remote(w_in.at[others], w_in.at[others], wp_send, k_recv, (row, peers[0])).wait_send()
 
     @pl.when(gives)
     def _():
@@ -1106,7 +1113,6 @@
             pltpu.SemaphoreType.REGULAR,
             pltpu.SemaphoreType.REGULAR,
             dma,
-            dma((n_col,)),
             dma, dma, dma, dma, dma,
             dma, dma, dma, dma, dma, dma, dma, dma, dma,
         ],

time: 28.6 us -> 28.5 us (level)
  no operation moved by 1% of the time
where the time goes in v8:
time: 28.5 us; the launch traced here: 28 us
  Pallas kernels  26.3 us (92%)
  local copies, waits for them, and re-layouts  1.12 us (4%)
  between operations  0.64 us (2%)
    pallas_call x1, Pallas kernels, local(): pl.pallas_call(functools.partial(kernel, n_row, n_col), out_shape=(pltpu....  26.3 us
    unnamed x2, local copies, waits for them, and re-layouts  1.12 us

profile of v8, /device:TPU:25, one launch (start us, length us, event | category | flops | bytes accessed | tf_op | source)
XLA Modules:
  0.0 28.0 jit_solution(8234303414495984850)
XLA Ops:
  0.6 26.3 %forward_solve.1 = (f32[1,1,4,1024]{3,2,1,0:T(4,128)S(1)}, f32[1,1,4]{2,1,0:T(1,128)S(1)}) custom-call(f32[1,1,4,1024]{3,2,1,0:T(4,128)} %rhs_hbm.1, bf16[1,1,256,1024]{3,2,1,0:T(8,128)(2,1)} %inv_hbm.1, bf16[1,1,2,1,128,1024]{5,4,3,2,1,0:T(8,128)(2,1)} %u_hbm.1, bf16[1,1,2,1,128,1024]{5,4,3,2,1,0:T(8,128)(2,1)} %v_hbm.1, s32[2]{0:T(128)} %bitcast.1), custom_call_target="tpu_custom_call" | custom-call | tf_op jit(solution)/shard_map/forward_solve/pallas_call | solution.py:1049
  26.9 0.6 %copy.9 = f32[1,1,4,1024]{3,2,1,0:T(4,128)} copy(f32[1,1,4,1024]{3,2,1,0:T(4,128)S(1)} %get-tuple-element.2) | data formatting | bytes 32768
  27.5 0.5 %copy.10 = f32[1,1,4]{2,1,0:T(1,128)} copy(f32[1,1,4]{2,1,0:T(1,128)S(1)} %get-tuple-element.3) | data formatting | bytes 32

commit v9 on v8

--- a/solution.py
+++ b/solution.py
@@ -39,7 +39,7 @@
     in_sem, y_send, y_recv, p_send, p_recv, o_send, o_recv, l_send, l_recv,
     v_send, v_recv, u_send, u_recv, w_send, w_recv, m_recv, f_send, e_send, ready, ready_far, pass_send,
     t_recv, k_recv, d_send, d_recv, du_recv, wl_send, wl_recv, wp_send,
-    we_send, we_recv, wx_send, wm_recv, a_send, a_recv,
+    we_send, we_recv, wx_send, wx_recv, a_send, a_recv,
 ):
     row = lax.axis_index("row")
     col = lax.axis_index("col")
@@ -505,7 +505,7 @@
         return remote(src, dst, send, recv, (row + 1, col))
 
     def lend_inverse(c):
-        return lend(hv_out.at[:, tail_of(c)], hv_in.at[:, tail_of(c)], wl_send, wm_recv)
+        return lend(hv_out.at[:, tail_of(c)], hv_in.at[:, tail_of(c)], wl_send, wx_recv)
 
     def lend_tail(c):
         hv_out[:, tail_of(c)] = inv_ref[:, tail_of(c)].astype(jnp.float32)
@@ -678,7 +678,7 @@
     @pl.when(is_ahead)
     def _():
         back = (row - 1, col)
-        by_col(lambda c: remote(hv_in.at[:, tail_of(c)], hv_in.at[:, tail_of(c)], wl_send, wm_recv, back).wait_recv())
+        by_col(lambda c: remote(hv_in.at[:, tail_of(c)], hv_in.at[:, tail_of(c)], wl_send, wx_recv, back).wait_recv())
         by_col(lambda c: hv_tile.__setitem__((slice(None), tail_of(c)), hv_in[:, tail_of(c)].astype(jnp.bfloat16)))
         remote(hl_in, hl_in, a_send, k_recv, back).wait_recv()
         remote(hu_in, hu_in, we_send, a_recv, back).wait_recv()
@@ -754,7 +754,7 @@
 
         return acc - p_in[j]
 
-    base[...] = lax.fori_loop(0, long_count, gather_p, base[...])
+    base[...] = lax.fori_loop(0, long_count - jnp.where(is_ahead, 1, 0), gather_p, base[...])
 
     @pl.when(lent)
     def _():
@@ -799,7 +799,8 @@
         inner = w_in[0]
         for s in range(1, n_col):
             inner = inner + w_in[s]
-        base[...] -= jnp.dot(inner.astype(jnp.bfloat16), u_part, preferred_element_type=jnp.float32)
+        part = base[...] - jnp.dot(inner.astype(jnp.bfloat16), u_part, preferred_element_type=jnp.float32)
+        base[...] = gather_p(row - 2, part)
 
     @pl.when(short & jnp.logical_not(is_end | is_ahead | lent))
     def _():
@@ -817,6 +818,8 @@
         shared_wait(t_in, t_recv, far_home)
         u_part = u_in[...].astype(jnp.bfloat16)
         t_part = t_in[...].astype(jnp.bfloat16)
+        carried = -jnp.dot(a_sum[0], u_part, preferred_element_type=jnp.float32)
+        both = jnp.concatenate([carried.astype(jnp.bfloat16), t_part])
 
         @pl.when(jnp.logical_not(takes))
         def _():
@@ -829,11 +832,10 @@
         inner = wait_w(w_in, w_send, w_recv, row - 1)
         inner -= jnp.dot(w2_in[...].astype(jnp.bfloat16), a_sum[2], preferred_element_type=jnp.float32)
         inner -= jnp.dot(wl_in[...].astype(jnp.bfloat16), a_sum[1], preferred_element_type=jnp.float32)
-        late = wait_w(wx_in, wx_send, wm_recv, row - 2)
-        base[...] -= jnp.dot(late.astype(jnp.bfloat16), t_part, preferred_element_type=jnp.float32)
-        late = wait_w(we_in, we_send, we_recv, row - 2)
-        inner -= jnp.dot(late.astype(jnp.bfloat16), a_sum[0], preferred_element_type=jnp.float32)
-        base[...] -= jnp.dot(inner.astype(jnp.bfloat16), u_part, preferred_element_type=jnp.float32)
+        part = base[...] - jnp.dot(inner.astype(jnp.bfloat16), u_part, preferred_element_type=jnp.float32)
+        late = [wait_w(we_in, we_send, we_recv, row - 2), wait_w(wx_in, wx_send, wx_recv, row - 2)]
+        late = jnp.concatenate(late, axis=1).astype(jnp.bfloat16)
+        base[...] = part - jnp.dot(late, both, preferred_element_type=jnp.float32)
 
     reduced = base[...].astype(jnp.bfloat16)
 
@@ -850,7 +852,7 @@
             send_w(w_out, w_in, w_send, w_recv, row + 1)
             send_w(w_out, we_in, we_send, we_recv, row + 2)
             wx_out[...] = jnp.dot(reduced, fold_x[...].astype(jnp.bfloat16), preferred_element_type=jnp.float32)
-            send_w(wx_out, wx_in, wx_send, wm_recv, row + 2)
+            send_w(wx_out, wx_in, wx_send, wx_recv, row + 2)
 
         @pl.when(before)
         def _():
@@ -917,7 +919,7 @@
         by_col(lambda c: borrowed_y(c).wait_send())
         remote(hz_out, hz_in, wl_send, du_recv, (row - 1, col)).wait_send()
         remote(w_in, w_in, we_send, we_recv, (row + 2, 0)).wait_send()
-        remote(w_in, w_in, wx_send, wm_recv, (row + 2, 0)).wait_send()
+        remote(w_in, w_in, wx_send, wx_recv, (row + 2, 0)).wait_send()
 
     @pl.when(is_even_end)
     def _():

time: 28.5 us -> 28.4 us (level)
  no operation moved by 1% of the time
where the time goes in v9:
time: 28.4 us; the launch traced here: 28.1 us
  Pallas kernels  26.3 us (93%)
  local copies, waits for them, and re-layouts  1.12 us (4%)
  between operations  0.64 us (2%)
    pallas_call x1, Pallas kernels, local(): pl.pallas_call(functools.partial(kernel, n_row, n_col), out_shape=(pltpu....  26.3 us
    unnamed x2, local copies, waits for them, and re-layouts  1.12 us

profile of v9, /device:TPU:25, one launch (start us, length us, event | category | flops | bytes accessed | tf_op | source)
XLA Modules:
  0.0 28.1 jit_solution(4732259126561435994)
XLA Ops:
  0.6 26.3 %forward_solve.1 = (f32[1,1,4,1024]{3,2,1,0:T(4,128)S(1)}, f32[1,1,4]{2,1,0:T(1,128)S(1)}) custom-call(f32[1,1,4,1024]{3,2,1,0:T(4,128)} %rhs_hbm.1, bf16[1,1,256,1024]{3,2,1,0:T(8,128)(2,1)} %inv_hbm.1, bf16[1,1,2,1,128,1024]{5,4,3,2,1,0:T(8,128)(2,1)} %u_hbm.1, bf16[1,1,2,1,128,1024]{5,4,3,2,1,0:T(8,128)(2,1)} %v_hbm.1, s32[2]{0:T(128)} %bitcast.1), custom_call_target="tpu_custom_call" | custom-call | tf_op jit(solution)/shard_map/forward_solve/pallas_call | solution.py:1051
  27.0 0.6 %copy.9 = f32[1,1,4,1024]{3,2,1,0:T(4,128)} copy(f32[1,1,4,1024]{3,2,1,0:T(4,128)S(1)} %get-tuple-element.2) | data formatting | bytes 32768
  27.6 0.5 %copy.10 = f32[1,1,4]{2,1,0:T(1,128)} copy(f32[1,1,4]{2,1,0:T(1,128)S(1)} %get-tuple-element.3) | data formatting | bytes 32

commit v10 on v9

--- a/solution.py
+++ b/solution.py
@@ -35,7 +35,7 @@
     x_out, x_in, t_out, t_in, fold_x, wx_out, wx_in,
     d_out, d_in, d_tile, vt_ref, l2_in, w2_out, w2_in, l_out, l_in, wl_out, wl_in, we_in,
     a_out, a_in, a_sum,
-    hl_in, hu_in, hf_in, hv_out, hv_in, hv_tile, hb_out, hb_in, hz_out, hz_in, hw_out, hw_in, hy_out,
+    hl_in, hu_in, hf_in, hv_out, hv_in, hv_tile, hb_out, hb_in, hz_out, hz_in, hw_out, hw_in, hy_out, fold_b, fold_xb,
     in_sem, y_send, y_recv, p_send, p_recv, o_send, o_recv, l_send, l_recv,
     v_send, v_recv, u_send, u_recv, w_send, w_recv, m_recv, f_send, e_send, ready, ready_far, pass_send,
     t_recv, k_recv, d_send, d_recv, du_recv, wl_send, wl_recv, wp_send,
@@ -622,6 +622,7 @@
     def products():
         fold_with(v_in, v_recv, fold)
         factor = fold[...].astype(jnp.bfloat16)
+        fold_b[...] = factor
         shared_wait(u_in, u_recv, prev_home)
         shared_wait(l_in, k_recv, mine_home)
         a_out[0] = jnp.dot(u_in[...].astype(jnp.bfloat16), factor, preferred_element_type=jnp.float32)
@@ -722,6 +723,7 @@
     @pl.when(feeds & jnp.logical_not(is_even_end))
     def _():
         fold_with(v_in, v_recv, fold)
+        fold_b[...] = fold[...].astype(jnp.bfloat16)
 
         @pl.when(lent)
         def _():
@@ -735,6 +737,7 @@
     @pl.when(is_ahead)
     def _():
         fold_with(x_in, m_recv, fold_x)
+        fold_xb[...] = fold_x[...].astype(jnp.bfloat16)
 
     @pl.when(is_end)
     def _():
@@ -769,7 +772,7 @@
 
     @pl.when(is_even_end)
     def _():
-        w_out[...] = jnp.dot(base[...].astype(jnp.bfloat16), fold[...].astype(jnp.bfloat16), preferred_element_type=jnp.float32)
+        w_out[...] = jnp.dot(base[...].astype(jnp.bfloat16), fold_b[...], preferred_element_type=jnp.float32)
         send_w(w_out, w_in, w_send, w_recv, row + 1)
 
     @pl.when(handed & jnp.logical_not(lent))
@@ -845,13 +848,13 @@
 
     @pl.when(feeds & jnp.logical_not(is_even_end | lent))
     def _():
-        w_out[...] = jnp.dot(reduced, fold[...].astype(jnp.bfloat16), preferred_element_type=jnp.float32)
+        w_out[...] = jnp.dot(reduced, fold_b[...], preferred_element_type=jnp.float32)
 
         @pl.when(is_ahead)
         def _():
             send_w(w_out, w_in, w_send, w_recv, row + 1)
             send_w(w_out, we_in, we_send, we_recv, row + 2)
-            wx_out[...] = jnp.dot(reduced, fold_x[...].astype(jnp.bfloat16), preferred_element_type=jnp.float32)
+            wx_out[...] = jnp.dot(reduced, fold_xb[...], preferred_element_type=jnp.float32)
             send_w(wx_out, wx_in, wx_send, wx_recv, row + 2)
 
         @pl.when(before)
@@ -1101,6 +1104,8 @@
             f32(nrhs, rank_max),
             f32(n_col, nrhs, rank_max),
             f32(nrhs, width),
+            bf16(piece, rank_max),
+            bf16(piece, rank_max),
             dma((5,)),
             dma((max(NEAR + 1, n_row - NEAR - 1),)),
             dma((per_col,)),

time: 28.4 us -> 28.4 us (level)
  no operation moved by 1% of the time
where the time goes in v10:
time: 28.4 us; the launch traced here: 28.1 us
  Pallas kernels  26.3 us (93%)
  local copies, waits for them, and re-layouts  1.12 us (4%)
  between operations  0.64 us (2%)
    pallas_call x1, Pallas kernels, local(): pl.pallas_call(functools.partial(kernel, n_row, n_col), out_shape=(pltpu....  26.3 us
    unnamed x2, local copies, waits for them, and re-layouts  1.12 us

profile of v10, /device:TPU:25, one launch (start us, length us, event | category | flops | bytes accessed | tf_op | source)
XLA Modules:
  0.0 28.1 jit_solution(17429634268590798712)
XLA Ops:
  0.6 26.3 %forward_solve.1 = (f32[1,1,4,1024]{3,2,1,0:T(4,128)S(1)}, f32[1,1,4]{2,1,0:T(1,128)S(1)}) custom-call(f32[1,1,4,1024]{3,2,1,0:T(4,128)} %rhs_hbm.1, bf16[1,1,256,1024]{3,2,1,0:T(8,128)(2,1)} %inv_hbm.1, bf16[1,1,2,1,128,1024]{5,4,3,2,1,0:T(8,128)(2,1)} %u_hbm.1, bf16[1,1,2,1,128,1024]{5,4,3,2,1,0:T(8,128)(2,1)} %v_hbm.1, s32[2]{0:T(128)} %bitcast.1), custom_call_target="tpu_custom_call" | custom-call | tf_op jit(solution)/shard_map/forward_solve/pallas_call | solution.py:1054
  27.0 0.6 %copy.9 = f32[1,1,4,1024]{3,2,1,0:T(4,128)} copy(f32[1,1,4,1024]{3,2,1,0:T(4,128)S(1)} %get-tuple-element.2) | data formatting | bytes 32768
  27.6 0.5 %copy.10 = f32[1,1,4]{2,1,0:T(1,128)} copy(f32[1,1,4]{2,1,0:T(1,128)S(1)} %get-tuple-element.3) | data formatting | bytes 32
